TPU v7x, 32 devices: a whole 2x2x4 slice. The times are simulated.
32 devices in a mesh: seq: 4 (over y, x), dp: 8 (over z, core).
Axes of the slice: x: 2, y: 2, z: 4, core: 2. Of those that a mesh axis runs over, the one named last changes fastest.
Arguments:
- hidden_in: bfloat16 [8, 2048, 768], P('dp', 'seq'), may hold values from -6 to 6
- seq_lengths: int32 [8], P('dp'), may hold values from 128 to 2048, as said below
- attention_gain: float32 [768], replicated, may hold values from 0.1 to 1.9
- attention_shift: float32 [768], replicated, may hold values from -3 to 3
- feed_gain: float32 [768], replicated, may hold values from 0.1 to 1.9
- feed_shift: float32 [768], replicated, may hold values from -3 to 3
- query_weight: bfloat16 [768, 768], replicated, may hold values from -0.21875 to 0.21875
- query_bias: float32 [768], replicated, may hold values from -3 to 3
- keyval_weight: bfloat16 [768, 128], replicated, may hold values from -0.21875 to 0.21875
- keyval_bias: float32 [128], replicated, may hold values from -3 to 3
- dense_weight: bfloat16 [768, 768], replicated, may hold values from -1.75 to 1.75
- dense_bias: float32 [768], replicated, may hold values from -3 to 3
- expand_weight: bfloat16 [768, 3072], replicated, may hold values from -0.21875 to 0.21875
- expand_bias: float32 [3072], replicated, may hold values from -3 to 3
- project_weight: bfloat16 [3072, 768], replicated, may hold values from -0.109375 to 0.109375
- project_bias: float32 [768], replicated, may hold values from -3 to 3
- out_grad: bfloat16 [8, 2048, 768], P('dp', 'seq'), may hold values from -6 to 6
Outputs:
- output: bfloat16 [8, 2048, 768], P('dp', 'seq')
- input_grad: float32 [8, 2048, 768], P('dp', 'seq')
- attention_gain_grad: float32 [768], replicated
- attention_shift_grad: float32 [768], replicated
- feed_gain_grad: float32 [768], replicated
- feed_shift_grad: float32 [768], replicated
- query_weight_grad: float32 [768, 768], P('dp', 'seq')
- query_bias_grad: float32 [768], replicated
- keyval_weight_grad: float32 [768, 128], P('dp', 'seq')
- keyval_bias_grad: float32 [128], replicated
- dense_weight_grad: float32 [768, 768], P('dp', 'seq')
- dense_bias_grad: float32 [768], replicated
- expand_weight_grad: float32 [768, 3072], P('dp', 'seq')
- expand_bias_grad: float32 [3072], replicated
- project_weight_grad: float32 [3072, 768], P('dp', 'seq')
- project_bias_grad: float32 [768], replicated
Inputs may be any that keep to these rules, and one draw needn't show every extreme that they name: `seq_lengths`: the valid tokens of a sequence are its first ones; in every draw one sequence fills all 2048 slots and one has exactly 128.
All inputs are finite; a program needn't handle non-finite values.
Results may differ from a plain program's by a relative error of at most 0.012.
Values may be sent and summed in bfloat16 or wider, within the bound.
A program may use at most 192 MiB of HBM per device.

v0:
```python
import jax
import jax.numpy as jnp
from jax import lax
from jax.sharding import PartitionSpec as P

HEADS = 12
HD = 64
ROT = 16


norm_eps = 1e-05
masked_score = -1e30


def layer_norm(values, gains, shifts):
    average = jnp.mean(values, axis=-1, keepdims=True)
    centered = values - average
    variance = jnp.mean(centered * centered, axis=-1, keepdims=True)
    return centered * lax.rsqrt(variance + norm_eps) * gains + shifts


def rotate(vectors, positions):
    half_rot = ROT // 2
    frequency = 10000.0 ** (-2.0 * jnp.arange(half_rot, dtype=jnp.float32) / ROT)
    angles = positions.astype(jnp.float32)[:, None] * frequency[None, :]
    cosine = jnp.cos(angles)
    sine_part = jnp.sin(angles)
    lead_part = vectors[..., :half_rot]
    pair_part = vectors[..., half_rot:ROT]
    rest_part = vectors[..., ROT:]
    return jnp.concatenate(
        [
            lead_part * cosine - pair_part * sine_part,
            pair_part * cosine + lead_part * sine_part,
            rest_part,
        ],
        axis=-1,
    )


def exact_gelu(values):
    return jax.nn.gelu(values, approximate=False)


def outer_sum(left, right):
    return lax.dot_general(
        left, right, (((0,), (0,)), ((), ())), preferred_element_type=jnp.float32
    )


def per_device(
    hidden_in,
    seq_lengths,
    attention_gain,
    attention_shift,
    feed_gain,
    feed_shift,
    query_weight,
    query_bias,
    keyval_weight,
    keyval_bias,
    dense_weight,
    dense_bias,
    expand_weight,
    expand_bias,
    project_weight,
    project_bias,
    out_grad,
):
    seq_count, stretch_len, model_width = hidden_in.shape
    seq_parts = lax.axis_size("seq")
    whole_len = stretch_len * seq_parts
    offset = lax.axis_index("seq") * stretch_len
    positions = offset + jnp.arange(stretch_len, dtype=jnp.int32)
    row_count = seq_count * stretch_len
    query_scale = HD ** (-0.5)
    inputs = hidden_in.astype(jnp.float32).reshape(row_count, model_width)
    valid_rows = positions[None, :] < seq_lengths[:, None]
    grad_out = jnp.where(valid_rows[:, :, None], out_grad, jnp.zeros_like(out_grad)).reshape(
        row_count, model_width
    )
    attn_norm, attn_norm_back = jax.vjp(layer_norm, inputs, attention_gain, attention_shift)
    feed_norm, feed_norm_back = jax.vjp(layer_norm, inputs, feed_gain, feed_shift)
    attn_in = attn_norm.astype(jnp.bfloat16)
    feed_in = feed_norm.astype(jnp.bfloat16)
    query_pre = jnp.dot(attn_in, query_weight, preferred_element_type=jnp.float32) + query_bias
    keyval_pre = jnp.dot(attn_in, keyval_weight, preferred_element_type=jnp.float32) + keyval_bias

    def turn_query(flat_query):
        shaped = flat_query.reshape(seq_count, stretch_len, HEADS, HD).transpose(0, 2, 1, 3)
        return rotate(shaped, positions) * query_scale

    def turn_keyval(flat_keyval):
        shaped = flat_keyval.reshape(seq_count, stretch_len, 2 * HD)
        return jnp.concatenate([rotate(shaped[..., :HD], positions), shaped[..., HD:]], axis=-1)

    query_rot, query_back = jax.vjp(turn_query, query_pre)
    keyval_rot, keyval_back = jax.vjp(turn_keyval, keyval_pre)
    query_low = query_rot.astype(jnp.bfloat16)
    keyval_low = keyval_rot.astype(jnp.bfloat16)
    gathered = lax.all_gather(keyval_low, "seq", axis=1, tiled=True)
    grad_mixed = jnp.dot(grad_out, dense_weight.T, preferred_element_type=jnp.float32).astype(
        jnp.bfloat16
    )
    grad_heads = grad_mixed.reshape(seq_count, stretch_len, HEADS, HD).transpose(0, 2, 1, 3)
    key_block = min(512, whole_len)
    block_count = whole_len // key_block
    group_size = 4

    def attend(operands):
        query_seq, grad_seq, keyval_seq, length = operands
        extent = block_count * key_block
        key_rows = keyval_seq[:extent, :HD]
        values = keyval_seq[:extent, HD:]
        key_pos = jnp.arange(extent, dtype=jnp.int32)
        allowed = (key_pos[None, :] <= positions[:, None]) & (key_pos[None, :] < length)

        def one_group(group_pair):
            query_grp, grad_grp = group_pair
            scores = jnp.einsum(
                "gtd,sd->gts", query_grp, key_rows, preferred_element_type=jnp.float32
            )
            scores = jnp.where(allowed[None], scores, masked_score)
            log_total = jax.nn.logsumexp(scores, axis=-1, keepdims=True)
            soft_weights = jnp.exp(scores - log_total)
            soft_low = soft_weights.astype(jnp.bfloat16)
            mixed_part = jnp.einsum(
                "gts,sd->gtd", soft_low, values, preferred_element_type=jnp.float32
            )
            grad_soft = jnp.einsum(
                "gtd,sd->gts", grad_grp, values, preferred_element_type=jnp.float32
            )
            row_delta = jnp.sum(soft_weights * grad_soft, axis=-1, keepdims=True)
            grad_scores = (soft_weights * (grad_soft - row_delta)).astype(jnp.bfloat16)
            grad_query = jnp.einsum(
                "gts,sd->gtd", grad_scores, key_rows, preferred_element_type=jnp.float32
            )
            grad_keys = jnp.einsum(
                "gts,gtd->sd", grad_scores, query_grp, preferred_element_type=jnp.float32
            )
            grad_values = jnp.einsum(
                "gts,gtd->sd", soft_low, grad_grp, preferred_element_type=jnp.float32
            )
            return (mixed_part, grad_query, jnp.concatenate([grad_keys, grad_values], axis=-1))

        grouped_query = query_seq.reshape(HEADS // group_size, group_size, stretch_len, HD)
        grouped_grad = grad_seq.reshape(HEADS // group_size, group_size, stretch_len, HD)
        mixed_part, grad_query, grad_keyval = lax.map(one_group, (grouped_query, grouped_grad))
        grad_keyval = jnp.sum(grad_keyval, axis=0)
        return (
            mixed_part.reshape(HEADS, stretch_len, HD),
            grad_query.reshape(HEADS, stretch_len, HD),
            grad_keyval,
        )

    mixed_all, grad_query_all, grad_keyval_all = lax.map(
        attend, (query_low, grad_heads, gathered, seq_lengths)
    )
    grad_keyval_own = lax.psum_scatter(grad_keyval_all, "seq", scatter_dimension=1, tiled=True)
    mixed_low = mixed_all.transpose(0, 2, 1, 3).reshape(row_count, model_width).astype(jnp.bfloat16)
    attn_out = jnp.dot(mixed_low, dense_weight, preferred_element_type=jnp.float32) + dense_bias
    upper = jnp.dot(feed_in, expand_weight, preferred_element_type=jnp.float32) + expand_bias
    active, active_back = jax.vjp(exact_gelu, upper)
    active_low = active.astype(jnp.bfloat16)
    feed_out = (
        jnp.dot(active_low, project_weight, preferred_element_type=jnp.float32) + project_bias
    )
    output = (
        (inputs + attn_out + feed_out)
        .astype(jnp.bfloat16)
        .reshape(seq_count, stretch_len, model_width)
    )
    grad_active = jnp.dot(grad_out, project_weight.T, preferred_element_type=jnp.float32)
    grad_upper = active_back(grad_active)[0].astype(jnp.bfloat16)
    grad_query_pre = query_back(grad_query_all)[0].astype(jnp.bfloat16)
    grad_keyval_pre = keyval_back(grad_keyval_own)[0].astype(jnp.bfloat16)
    grad_attn_in = jnp.dot(
        grad_query_pre, query_weight.T, preferred_element_type=jnp.float32
    ) + jnp.dot(grad_keyval_pre, keyval_weight.T, preferred_element_type=jnp.float32)
    grad_feed_in = jnp.dot(grad_upper, expand_weight.T, preferred_element_type=jnp.float32)
    attn_dx, attn_dgain, attn_dshift = attn_norm_back(grad_attn_in)
    feed_dx, feed_dgain, feed_dshift = feed_norm_back(grad_feed_in)
    input_grad = (grad_out.astype(jnp.float32) + attn_dx + feed_dx).reshape(
        seq_count, stretch_len, model_width
    )
    query_term = outer_sum(attn_in, grad_query_pre)
    keyval_term = outer_sum(attn_in, grad_keyval_pre)
    dense_term = outer_sum(mixed_low, grad_out)
    expand_term = outer_sum(feed_in, grad_upper)
    project_term = outer_sum(active_low, grad_out)
    row_sums = (
        lax.psum_scatter(query_term, "dp", scatter_dimension=0, tiled=True),
        lax.psum_scatter(keyval_term, "dp", scatter_dimension=0, tiled=True),
        lax.psum_scatter(dense_term, "dp", scatter_dimension=0, tiled=True),
        lax.psum_scatter(expand_term, "dp", scatter_dimension=0, tiled=True),
        lax.psum_scatter(project_term, "dp", scatter_dimension=0, tiled=True),
    )
    weight_grads = (
        lax.psum_scatter(row_sums[0], "seq", scatter_dimension=1, tiled=True),
        lax.psum_scatter(row_sums[1], "seq", scatter_dimension=1, tiled=True),
        lax.psum_scatter(row_sums[2], "seq", scatter_dimension=1, tiled=True),
        lax.psum_scatter(row_sums[3], "seq", scatter_dimension=1, tiled=True),
        lax.psum_scatter(row_sums[4], "seq", scatter_dimension=1, tiled=True),
    )
    out_total = jnp.sum(grad_out, axis=0, dtype=jnp.float32)
    small_sums = lax.psum(
        (
            attn_dgain,
            attn_dshift,
            feed_dgain,
            feed_dshift,
            jnp.sum(grad_query_pre, axis=0, dtype=jnp.float32),
            jnp.sum(grad_keyval_pre, axis=0, dtype=jnp.float32),
            out_total,
            jnp.sum(grad_upper, axis=0, dtype=jnp.float32),
        ),
        ("seq", "dp"),
    )
    return (
        output,
        input_grad,
        small_sums[0],
        small_sums[1],
        small_sums[2],
        small_sums[3],
        weight_grads[0],
        small_sums[4],
        weight_grads[1],
        small_sums[5],
        weight_grads[2],
        small_sums[6],
        weight_grads[3],
        small_sums[7],
        weight_grads[4],
        small_sums[6],
    )


def solution(mesh):
    return jax.shard_map(
        per_device,
        mesh=mesh,
        in_specs=(
            P("dp", "seq", None),
            P("dp"),
            P(),
            P(),
            P(),
            P(),
            P(),
            P(),
            P(),
            P(),
            P(),
            P(),
            P(),
            P(),
            P(),
            P(),
            P("dp", "seq", None),
        ),
        out_specs=(
            P("dp", "seq", None),
            P("dp", "seq", None),
            P(),
            P(),
            P(),
            P(),
            P("dp", "seq"),
            P(),
            P("dp", "seq"),
            P(),
            P("dp", "seq"),
            P(),
            P("dp", "seq"),
            P(),
            P("dp", "seq"),
            P(),
        ),
        check_vma=False,
    )
```

profile of v0, /device:TPU:0, one launch (start us, length us, event | category | flops | bytes accessed | tf_op | source)
XLA Modules:
  0.0 712.5 jit_solution(7494553128923703508)
XLA Ops:
  21.3 11.5 %all_gather.3 = bf16[1,2048,128]{1,2,0:T(8,128)(2,1)S(1)} all-gather(bf16[1,512,128]{1,2,0:T(8,128)(2,1)S(1)} %pad_maximum_fusion), channel_id=1, replica_groups=mesh['seq'=4,'dp'=8] {'seq'}, dimensions={1}, use_global_device_ids=true | all-gather | bytes 655360 | tf_op jit(solution)/shard_map/all_gather | solution.py:101
  37.8 180.2 %while.26 = (s32[]{:T(128)}, bf16[3,4,512,64]{2,3,1,0:T(8,128)(2,1)}, f32[3,4,512,64]{2,3,1,0:T(8,128)}, f32[3,2048,128]{1,2,0:T(8,128)}, bf16[3,4,512,64]{2,3,1...) while((s32[]{:T(128)}, ...), condition=%wide.region_6.7_spmd.clone, body=%wide.region_2.6_spmd.clone.sunk | while | flops 3307476992 | bytes 290576096 | solution.py:148
  38.7 2.7 select_reduce_fusion.2
  41.4 4.0 exponential_reduce_fusion.2
  47.2 12.8 %multiply_reduce_fusion.2 = (f32[4,512]{1,0:T(4,128)S(1)}, f32[4,512,2048]{2,1,0:T(8,128)}) fusion(f32[4,512,2048]{2,1,0:T(8,128)} %copy-done.1, f32[4,512]{1,0:T(4,128)S(1)} %log_add_fusion.2, pred[512,2048]{1,0:T(8,128)(4,1)S(1)} %fusion.156, bf16[2048,64]{0,1:T(8,128)(2,1)S(1)} %get-tuple-element.334, ...), kind=kOutput, calls=%fused_computation.2.clone.1 | convolution fusion | flops 553646080 | bytes 35143684 | tf_op jit(solution)/shard_map/while/body/eval_jaxpr/while/body/eval_jaxpr/gtd,sd->gts/dot_general | solution.py:130
  60.0 16.0 %multiply_convert_fusion.3 = bf16[4,512,2048]{2,1,0:T(8,128)(2,1)} fusion(f32[4,512,2048]{2,1,0:T(8,128)} %get-tuple-element.304, f32[4,512,2048]{2,1,0:T(8,128)} %copy-done.1, f32[4,512]{1,0:T(4,128)S(1)} %get-tuple-element.305, f32[4,512]{1,0:T(4,128)S(1)} %log_add_fusion.2, pred[512,2048]{1,0:T(8,128)(4,1)S(1)} %fusion.156), kind=kLoop, calls=%fused_computation.1.clone.1 | loop fusion | flops 20971520 | bytes 43008000 | tf_op jit(solution)/shard_map/while/body/eval_jaxpr/while/body/eval_jaxpr/convert_element_type | solution.py:134
  76.0 4.9 convolution_bitcast_fusion.7
  81.0 4.2 convolution_bitcast_fusion.6
  86.3 6.8 fusion.158
  93.1 4.7 fusion.157
  98.6 2.7 select_reduce_fusion.2
  101.3 4.0 exponential_reduce_fusion.2
  107.1 12.8 %multiply_reduce_fusion.2 = (f32[4,512]{1,0:T(4,128)S(1)}, f32[4,512,2048]{2,1,0:T(8,128)}) fusion(f32[4,512,2048]{2,1,0:T(8,128)} %copy-done.1, f32[4,512]{1,0:T(4,128)S(1)} %log_add_fusion.2, pred[512,2048]{1,0:T(8,128)(4,1)S(1)} %fusion.156, bf16[2048,64]{0,1:T(8,128)(2,1)S(1)} %get-tuple-element.334, ...), kind=kOutput, calls=%fused_computation.2.clone.1 | convolution fusion | flops 553646080 | bytes 35143684 | tf_op jit(solution)/shard_map/while/body/eval_jaxpr/while/body/eval_jaxpr/gtd,sd->gts/dot_general | solution.py:130
  119.8 16.0 %multiply_convert_fusion.3 = bf16[4,512,2048]{2,1,0:T(8,128)(2,1)} fusion(f32[4,512,2048]{2,1,0:T(8,128)} %get-tuple-element.304, f32[4,512,2048]{2,1,0:T(8,128)} %copy-done.1, f32[4,512]{1,0:T(4,128)S(1)} %get-tuple-element.305, f32[4,512]{1,0:T(4,128)S(1)} %log_add_fusion.2, pred[512,2048]{1,0:T(8,128)(4,1)S(1)} %fusion.156), kind=kLoop, calls=%fused_computation.1.clone.1 | loop fusion | flops 20971520 | bytes 43008000 | tf_op jit(solution)/shard_map/while/body/eval_jaxpr/while/body/eval_jaxpr/convert_element_type | solution.py:134
  135.8 4.9 convolution_bitcast_fusion.7
  140.8 4.2 convolution_bitcast_fusion.6
  146.2 6.8 fusion.158
  153.0 4.7 fusion.157
  158.5 2.7 select_reduce_fusion.2
  161.2 4.0 exponential_reduce_fusion.2
  167.0 12.8 %multiply_reduce_fusion.2 = (f32[4,512]{1,0:T(4,128)S(1)}, f32[4,512,2048]{2,1,0:T(8,128)}) fusion(f32[4,512,2048]{2,1,0:T(8,128)} %copy-done.1, f32[4,512]{1,0:T(4,128)S(1)} %log_add_fusion.2, pred[512,2048]{1,0:T(8,128)(4,1)S(1)} %fusion.156, bf16[2048,64]{0,1:T(8,128)(2,1)S(1)} %get-tuple-element.334, ...), kind=kOutput, calls=%fused_computation.2.clone.1 | convolution fusion | flops 553646080 | bytes 35143684 | tf_op jit(solution)/shard_map/while/body/eval_jaxpr/while/body/eval_jaxpr/gtd,sd->gts/dot_general | solution.py:130
  179.7 16.0 %multiply_convert_fusion.3 = bf16[4,512,2048]{2,1,0:T(8,128)(2,1)} fusion(f32[4,512,2048]{2,1,0:T(8,128)} %get-tuple-element.304, f32[4,512,2048]{2,1,0:T(8,128)} %copy-done.1, f32[4,512]{1,0:T(4,128)S(1)} %get-tuple-element.305, f32[4,512]{1,0:T(4,128)S(1)} %log_add_fusion.2, pred[512,2048]{1,0:T(8,128)(4,1)S(1)} %fusion.156), kind=kLoop, calls=%fused_computation.1.clone.1 | loop fusion | flops 20971520 | bytes 43008000 | tf_op jit(solution)/shard_map/while/body/eval_jaxpr/while/body/eval_jaxpr/convert_element_type | solution.py:134
  195.7 4.9 convolution_bitcast_fusion.7
  200.7 4.2 convolution_bitcast_fusion.6
  206.0 6.8 fusion.158
  212.9 4.7 fusion.157
  218.0 3.2 reduce_sum.159
  225.0 2.6 fusion.106
  227.6 3.6 fusion.70
  231.3 19.8 %multiply_convert_fusion.1 = (bf16[512,3072]{1,0:T(8,128)(2,1)}, f32[512,3072]{1,0:T(8,128)}, f32[512,3072]{1,0:T(8,128)}) fusion(f32[3072]{0:T(1024)S(1)} %copy-done.35, bf16[768,3072]{1,0:T(8,128)(2,1)} %param.31, bf16[1,512,768]{2,1,0:T(8,128)(2,1)S(1)} %copy-done.3, f32[768]{0:T(1024)S(1)} %copy-done.20, f32[768]{0:T(1024)S(1)} %copy-done.12, ...), kind=kOutput, calls=%fused_computation.43 | convolution fusion | flops 2522087424 | bytes 21256192 | tf_op jit(solution)/shard_map/dot_general | solution.py:162
  256.0 9.4 %convert_reduce_fusion = (f32[3072]{0:T(1024)}, bf16[512,3072]{1,0:T(8,128)(2,1)S(1)}) fusion(f32[512,3072]{1,0:T(8,128)} %get-tuple-element.208, bf16[3072,768]{1,0:T(8,128)(2,1)} %param.33, bf16[1,512,768]{2,1,0:T(8,128)(2,1)S(1)} %copy-done.6, pred[512]{0:T(512)(128)(4,1)S(1)} %copy-done.32, f32[512,3072]{1,0:T(8,128)} %get-tuple-element.231, ...), kind=kOutput, calls=%fused_computation.41 | convolution fusion | flops 2443047936 | bytes 21258752 | tf_op jit(solution)/shard_map/dot_general | solution.py:173
  267.1 5.5 fusion.99
  272.8 8.3 %fusion.68 = f32[3072,768]{1,0:T(8,128)} fusion(bf16[512,3072]{1,0:T(8,128)(2,1)} %get-tuple-element.207, bf16[1,512,768]{2,1,0:T(8,128)(2,1)S(1)} %copy-done.6, pred[512]{0:T(512)(128)(4,1)S(1)} %copy-done.32), kind=kOutput, calls=%fused_computation.104 | convolution fusion | flops 2416312320 | bytes 13369856 | tf_op jit(solution)/shard_map/dot_general | solution.py:46
  281.2 7.9 %reduce-scatter.22.cloned.1.call-done = f32[96,768]{1,0:T(8,128)} async-done(((f32[768,768]{1,0:T(8,128)}), f32[96,768]{1,0:T(8,128)}) %reduce-scatter.22.cloned.1.call-update) | async-done | bytes 294928 | tf_op jit(solution)/shard_map/reduce_scatter | solution.py:192
  291.0 36.3 %reduce-scatter.26.cloned.1.call-done = f32[96,768]{1,0:T(8,128)} async-done(((f32[768,768]{1,0:T(8,128)}), f32[96,768]{1,0:T(8,128)}) %reduce-scatter.26.cloned.1.call-update) | async-done | bytes 294928 | tf_op jit(solution)/shard_map/reduce_scatter | solution.py:194
  329.3 30.7 %reduce-scatter.24.cloned.1.call-done = f32[96,128]{1,0:T(8,128)} async-done(((f32[768,128]{1,0:T(8,128)}), f32[96,128]{1,0:T(8,128)}) %reduce-scatter.24.cloned.1.call-update) | async-done | bytes 49168 | tf_op jit(solution)/shard_map/reduce_scatter | solution.py:193
  361.6 98.2 %reduce-scatter.28.cloned.1.call-done = f32[96,3072]{1,0:T(8,128)} async-done(((f32[768,3072]{1,0:T(8,128)}), f32[96,3072]{1,0:T(8,128)}) %reduce-scatter.28.cloned.1.call-update) | async-done | bytes 1179664 | tf_op jit(solution)/shard_map/reduce_scatter | solution.py:195
  459.8 6.1 fusion.115
  465.9 6.6 fusion.114
  472.5 87.4 %reduce-scatter.32.cloned.1.call-done = f32[384,768]{1,0:T(8,128)} async-done(((f32[3072,768]{1,0:T(8,128)}), f32[384,768]{1,0:T(8,128)}) %reduce-scatter.32.cloned.1.call-update) | async-done | bytes 1179664 | tf_op jit(solution)/shard_map/reduce_scatter | solution.py:196
  559.8 2.7 copy.56
  562.5 3.8 fusion.65
  570.7 3.1 fusion.111
  575.9 2.8 convert_reduce_fusion.2
  578.7 39.7 %all-reduce.8 = (f32[768]{0:T(1024)}, f32[768]{0:T(1024)}, f32[768]{0:T(1024)}, f32[768]{0:T(1024)}, f32[768]{0:T(1024)}, /*index=5*/f32[128]{0:T(128)}, f32[768]{0:T(1024)S(1)}, f32[3072]{0:T(1024)}) all-reduce(f32[768]{0:T(1024)} %get-tuple-element.176, f32[768]{0:T(1024)} %get-tuple-element.173, ...), channel_id=1, replica_groups=mesh['seq'=4,'dp'=8] {'seq','dp'}, use_global_device_ids=true, to_apply=%region_14.15 | all-reduce | flops 7808 | bytes 62464 | tf_op jit(solution)/shard_map/psum | solution.py:206
  621.6 19.2 %reduce-scatter.36.cloned.1.call-done = f32[32,96]{1,0:T(8,128)} async-done(((f32[128,96]{1,0:T(8,128)}), f32[32,96]{1,0:T(8,128)}) %reduce-scatter.36.cloned.1.call-update) | async-done | bytes 12304
  640.9 32.1 %reduce-scatter.30.cloned.1.call-done = f32[96,768]{1,0:T(8,128)} async-done(((f32[96,3072]{1,0:T(8,128)}), f32[96,768]{1,0:T(8,128)}) %reduce-scatter.30.cloned.1.call-update) | async-done | bytes 294928 | tf_op jit(solution)/shard_map/reduce_scatter | solution.py:202
  673.0 32.2 %reduce-scatter.40.cloned.1.call-done = f32[192,384]{1,0:T(8,128)} async-done(((f32[768,384]{1,0:T(8,128)}), f32[192,384]{1,0:T(8,128)}) %reduce-scatter.40.cloned.1.call-update) | async-done | bytes 294928
  (194 shorter events, 55.2 us)
Async XLA Ops:
  7.2 7.8 %copy-start = (bf16[768,768]{1,0:T(8,128)(2,1)S(1)}, bf16[768,768]{1,0:T(8,128)(2,1)}, u32[]{:S(2)}) copy-start(bf16[768,768]{1,0:T(8,128)(2,1)} %param.25) | copy-start | bytes 3538948
  7.2 7.7 %copy-start.2 = (bf16[1,512,768]{2,1,0:T(8,128)(2,1)S(1)}, bf16[1,512,768]{2,1,0:T(8,128)(2,1)}, u32[]{:S(2)}) copy-start(bf16[1,512,768]{2,1,0:T(8,128)(2,1)} %param.19) | copy-start | bytes 2359300
  7.2 7.7 %copy-start.22 = (f32[768]{0:T(1024)S(1)}, f32[768]{0:T(1024)}, u32[]{:S(2)}) copy-start(f32[768]{0:T(1024)} %param.21) | copy-start | bytes 9220
  7.2 7.7 %copy-start.37 = (f32[768]{0:T(1024)S(1)}, f32[768]{0:T(1024)}, u32[]{:S(2)}) copy-start(f32[768]{0:T(1024)} %param.22) | copy-start | bytes 9220
  7.2 7.7 %copy-start.36 = (f32[768]{0:T(1024)S(1)}, f32[768]{0:T(1024)}, u32[]{:S(2)}) copy-start(f32[768]{0:T(1024)} %param.26) | copy-start | bytes 9220
  7.2 243.9 %reduce-scatter.20.cloned.1.call-start = ((), (), s32[]{:S(2)}) async-start(), calls=%async_computation.11 | async-start | bytes 1310720 | tf_op jit(solution)/shard_map/reduce_scatter | solution.py:159
  7.3 7.6 %copy-start.28 = (f32[8]{0:T(128)}, f32[8]{0:T(128)S(1)}, u32[]{:S(2)}) copy-start(f32[8]{0:T(128)S(1)} %multiply_power_fusion) | copy-start | bytes 100
  8.8 6.1 copy-start.13
  10.3 4.6 copy-start.15
  10.9 4.0 copy-start.24
  11.6 23.6 %copy-start.17 = (f32[512,8]{0,1:T(8,128)}, f32[512,8]{0,1:T(8,128)S(1)}, u32[]{:S(2)}) copy-start(f32[512,8]{0,1:T(8,128)S(1)} %get-tuple-element.227) | copy-start | bytes 49156
  17.0 17.0 %copy-start.5 = (bf16[1,512,768]{2,1,0:T(8,128)(2,1)S(1)}, bf16[1,512,768]{2,1,0:T(8,128)(2,1)}, u32[]{:S(2)}) copy-start(bf16[1,512,768]{2,1,0:T(8,128)(2,1)} %param.35) | copy-start | bytes 2359300
  19.0 13.8 %copy-start.4 = (f32[512,768]{0,1:T(8,128)}, f32[512,768]{0,1:T(8,128)S(1)}, u32[]{:S(2)}) copy-start(f32[512,768]{0,1:T(8,128)S(1)} %copy.46) | copy-start | bytes 4718596
  19.0 15.0 %copy-start.34 = (bf16[768,768]{1,0:T(8,128)(2,1)S(1)}, bf16[768,768]{1,0:T(8,128)(2,1)}, u32[]{:S(2)}) copy-start(bf16[768,768]{1,0:T(8,128)(2,1)} %param.29) | copy-start | bytes 3538948
  34.9 2.9 copy-start.21
  41.4 5.7 copy-start.1
  47.2 33.8 %slice-start = ((s8[16777216]{0:T(1024)(128)(4,1)}), s8[4194304]{0:T(1024)(128)(4,1)S(1)}, s32[]{:S(2)}) async-start(s8[16777216]{0:T(1024)(128)(4,1)} %bitcast.227), calls=%async_computation.22 | async-start | bytes 8388608 | tf_op jit(solution)/shard_map/while/body/eval_jaxpr/while
  47.2 33.8 %slice-start.1 = ((s8[16777216]{0:T(1024)(128)(4,1)}), s8[4194304]{0:T(1024)(128)(4,1)S(1)}, s32[]{:S(2)}) async-start(s8[16777216]{0:T(1024)(128)(4,1)} %bitcast.227), calls=%async_computation.23 | async-start | bytes 8388608 | tf_op jit(solution)/shard_map/while/body/eval_jaxpr/while
  60.0 21.0 %slice-start.2 = ((s8[16777216]{0:T(1024)(128)(4,1)}), s8[4194304]{0:T(1024)(128)(4,1)S(1)}, s32[]{:S(2)}) async-start(s8[16777216]{0:T(1024)(128)(4,1)} %bitcast.227), calls=%async_computation.24 | async-start | bytes 8388608 | tf_op jit(solution)/shard_map/while/body/eval_jaxpr/while
  60.0 21.0 %slice-start.3 = ((s8[16777216]{0:T(1024)(128)(4,1)}), s8[4194304]{0:T(1024)(128)(4,1)S(1)}, s32[]{:S(2)}) async-start(s8[16777216]{0:T(1024)(128)(4,1)} %bitcast.227), calls=%async_computation.25 | async-start | bytes 8388608 | tf_op jit(solution)/shard_map/while/body/eval_jaxpr/while
  101.3 5.7 copy-start.1
  107.0 33.8 %slice-start = ((s8[16777216]{0:T(1024)(128)(4,1)}), s8[4194304]{0:T(1024)(128)(4,1)S(1)}, s32[]{:S(2)}) async-start(s8[16777216]{0:T(1024)(128)(4,1)} %bitcast.227), calls=%async_computation.22 | async-start | bytes 8388608 | tf_op jit(solution)/shard_map/while/body/eval_jaxpr/while
  107.0 33.8 %slice-start.1 = ((s8[16777216]{0:T(1024)(128)(4,1)}), s8[4194304]{0:T(1024)(128)(4,1)S(1)}, s32[]{:S(2)}) async-start(s8[16777216]{0:T(1024)(128)(4,1)} %bitcast.227), calls=%async_computation.23 | async-start | bytes 8388608 | tf_op jit(solution)/shard_map/while/body/eval_jaxpr/while
  119.8 21.0 %slice-start.2 = ((s8[16777216]{0:T(1024)(128)(4,1)}), s8[4194304]{0:T(1024)(128)(4,1)S(1)}, s32[]{:S(2)}) async-start(s8[16777216]{0:T(1024)(128)(4,1)} %bitcast.227), calls=%async_computation.24 | async-start | bytes 8388608 | tf_op jit(solution)/shard_map/while/body/eval_jaxpr/while
  119.8 21.0 %slice-start.3 = ((s8[16777216]{0:T(1024)(128)(4,1)}), s8[4194304]{0:T(1024)(128)(4,1)S(1)}, s32[]{:S(2)}) async-start(s8[16777216]{0:T(1024)(128)(4,1)} %bitcast.227), calls=%async_computation.25 | async-start | bytes 8388608 | tf_op jit(solution)/shard_map/while/body/eval_jaxpr/while
  161.2 5.7 copy-start.1
  166.9 33.8 %slice-start = ((s8[16777216]{0:T(1024)(128)(4,1)}), s8[4194304]{0:T(1024)(128)(4,1)S(1)}, s32[]{:S(2)}) async-start(s8[16777216]{0:T(1024)(128)(4,1)} %bitcast.227), calls=%async_computation.22 | async-start | bytes 8388608 | tf_op jit(solution)/shard_map/while/body/eval_jaxpr/while
  166.9 33.8 %slice-start.1 = ((s8[16777216]{0:T(1024)(128)(4,1)}), s8[4194304]{0:T(1024)(128)(4,1)S(1)}, s32[]{:S(2)}) async-start(s8[16777216]{0:T(1024)(128)(4,1)} %bitcast.227), calls=%async_computation.23 | async-start | bytes 8388608 | tf_op jit(solution)/shard_map/while/body/eval_jaxpr/while
  179.7 21.0 %slice-start.2 = ((s8[16777216]{0:T(1024)(128)(4,1)}), s8[4194304]{0:T(1024)(128)(4,1)S(1)}, s32[]{:S(2)}) async-start(s8[16777216]{0:T(1024)(128)(4,1)} %bitcast.227), calls=%async_computation.24 | async-start | bytes 8388608 | tf_op jit(solution)/shard_map/while/body/eval_jaxpr/while
  179.7 21.0 %slice-start.3 = ((s8[16777216]{0:T(1024)(128)(4,1)}), s8[4194304]{0:T(1024)(128)(4,1)S(1)}, s32[]{:S(2)}) async-start(s8[16777216]{0:T(1024)(128)(4,1)} %bitcast.227), calls=%async_computation.25 | async-start | bytes 8388608 | tf_op jit(solution)/shard_map/while/body/eval_jaxpr/while
  221.2 67.8 %reduce-scatter.22.cloned.1.call-start = ((), (), s32[]{:S(2)}) async-start(), calls=%async_computation.12 | async-start | bytes 2654208 | tf_op jit(solution)/shard_map/reduce_scatter | solution.py:192
  227.5 99.8 %reduce-scatter.26.cloned.1.call-start = ((), (), s32[]{:S(2)}) async-start(), calls=%async_computation.14 | async-start | bytes 2654208 | tf_op jit(solution)/shard_map/reduce_scatter | solution.py:194
  227.6 3.7 copy-start.12
  227.6 3.7 copy-start.20
  227.6 3.7 copy-start.35
  231.2 21.7 %copy-start.25 = (f32[512]{0:T(512)S(1)}, f32[512]{0:T(512)}, u32[]{:S(2)}) copy-start(f32[512]{0:T(512)} %copy-done.24) | copy-start | bytes 6148
  231.2 21.7 %copy-start.29 = (f32[8]{0:T(128)S(1)}, f32[8]{0:T(128)}, u32[]{:S(2)}) copy-start(f32[8]{0:T(128)} %copy-done.28) | copy-start | bytes 100
  231.3 128.7 %reduce-scatter.24.cloned.1.call-start = ((), (), s32[]{:S(2)}) async-start(), calls=%async_computation.13 | async-start | bytes 442368 | tf_op jit(solution)/shard_map/reduce_scatter | solution.py:193
  256.0 203.8 %reduce-scatter.28.cloned.1.call-start = ((), (), s32[]{:S(2)}) async-start(), calls=%async_computation.15 | async-start | bytes 10616832 | tf_op jit(solution)/shard_map/reduce_scatter | solution.py:195
  272.6 287.2 %reduce-scatter.32.cloned.1.call-start = ((), (), s32[]{:S(2)}) async-start(), calls=%async_computation.17 | async-start | bytes 10616832 | tf_op jit(solution)/shard_map/reduce_scatter | solution.py:196
  281.1 337.2 %reduce-scatter.34.cloned.1.call-start = ((), (), s32[]{:S(2)}) async-start(), calls=%async_computation.18 | async-start | bytes 491520
  291.0 329.0 %reduce-scatter.38.cloned.1.call-start = ((), (), s32[]{:S(2)}) async-start(), calls=%async_computation.20 | async-start | bytes 491520
  329.2 311.7 %reduce-scatter.36.cloned.1.call-start = ((), (), s32[]{:S(2)}) async-start(), calls=%async_computation.19 | async-start | bytes 81920
  361.5 311.4 %reduce-scatter.30.cloned.1.call-start = ((), (), s32[]{:S(2)}) async-start(), calls=%async_computation.16 | async-start | bytes 1474560 | tf_op jit(solution)/shard_map/reduce_scatter | solution.py:202
  459.8 245.4 %reduce-scatter.40.cloned.1.call-start = ((), (), s32[]{:S(2)}) async-start(), calls=%async_computation.21 | async-start | bytes 1474560
  459.8 6.1 copy-start.39
  570.7 3.2 copy-start.27
  618.4 87.4 %copy-start.30 = (f32[768]{0:T(1024)}, f32[768]{0:T(1024)S(1)}, u32[]{:S(2)}) copy-start(f32[768]{0:T(1024)S(1)} %get-tuple-element.370) | copy-start | bytes 9220
  (17 other events, 28.3 us)
Sparse Core Ops, SparseCore 0:
  221.3 28.2 reduce-scatter.19
  251.9 37.0 reduce-scatter.21
  291.4 35.9 reduce-scatter.25
  330.0 29.9 reduce-scatter.23
  362.1 97.5 reduce-scatter.27
  461.9 97.8 reduce-scatter.31
  562.6 23.1 reduce-scatter.33
  588.6 24.7 reduce-scatter.37
  616.8 24.0 reduce-scatter.35
  644.2 28.6 reduce-scatter.29
  676.4 28.6 reduce-scatter.39
where the time goes:
time: 717 us; the launch traced here: 713 us
  waiting for transfers between devices  344 us (48%)
  matrix products  185 us (26%)
  other arithmetic  87.4 us (12%)
  blocking collectives  51.2 us (7%)
  local copies, waits for them, and re-layouts  28.1 us (4%)
  between operations  15.3 us (2%)
    reduce_scatter x1, waiting for transfers between devices, per_device(): lax.psum_scatter(expand_term, 'dp', scatter_dimension=0, tiled=True)  98.2 us
    reduce_scatter x1, waiting for transfers between devices, per_device(): lax.psum_scatter(project_term, 'dp', scatter_dimension=0, tiled=True)  87.4 us
    unnamed x15, waiting for transfers between devices  51.7 us
    convert_element_type x3, other arithmetic, one_group(): grad_scores = (soft_weights * (grad_soft - row_delta)).astype(jnp.bfloat16)  48 us
    psum x1, blocking collectives, per_device(): lax.psum((attn_dgain, attn_dshift, feed_dgain, feed_dshift, jnp.sum(grad_...  39.7 us
    dot_general x3, matrix products, one_group(): jnp.einsum('gtd,sd->gts', grad_grp, values, preferred_element_type=jnp.fl...  38.3 us
    reduce_scatter x1, waiting for transfers between devices, per_device(): lax.psum_scatter(dense_term, 'dp', scatter_dimension=0, tiled=True)  36.3 us
    reduce_scatter x1, waiting for transfers between devices, per_device(): lax.psum_scatter(row_sums[3], 'seq', scatter_dimension=1, tiled=True)  32.1 us
  transfers between devices with their start and end apart: 11, of which 8 were waited for; matrix products, arithmetic and copies ran while one was open for 13% of the time, Pallas kernels for 0%

commit v1 on v0

--- a/solution.py
+++ b/solution.py
@@ -1,11 +1,17 @@
+import functools
+
 import jax
 import jax.numpy as jnp
 from jax import lax
+from jax.experimental import pallas as pl
+from jax.experimental.pallas import tpu as pltpu
 from jax.sharding import PartitionSpec as P
 
 HEADS = 12
 HD = 64
 ROT = 16
+f32 = jnp.float32
+bf16 = jnp.bfloat16
 
 
 norm_eps = 1e-05
@@ -236,9 +242,401 @@
     )
 
 
+NT_DIMS = (((1,), (1,)), ((), ()))
+MESH_ID = pl.DeviceIdType.MESH
+
+
+def attend_kernel(
+    seq_parts, half_parts, q_ref, gm_ref, kaug_ref, val_ref, kvt_ref, ge_ref, gp_ref,
+    mix_ref, dq_ref, dkv_ref, oute_ref, outp_ref,
+    score, expo, qaug, pair, core_e, core_p, plane_e, plane_p, part_e, part_p, line_e, line_p,
+    core_send, core_recv, es_send, es_recv, ps_send, ps_recv, ez_send, ez_recv, pz_send, pz_recv,
+):
+    width, stretch = q_ref.shape
+    whole_len = kaug_ref.shape[0]
+    blocks = whole_len // stretch
+    seq = lax.axis_index("seq")
+    dp = lax.axis_index("dp")
+    core = lax.rem(dp, 2)
+    line = lax.div(dp, 2)
+    e_rows, e_cols = oute_ref.shape
+    p_rows, p_cols = outp_ref.shape
+
+    def seq_of(step):
+        return lax.rem(seq + step, seq_parts)
+
+    def line_of(step):
+        return lax.rem(line + step, half_parts)
+
+    barrier = pltpu.get_barrier_semaphore()
+    pl.semaphore_signal(barrier, inc=1, device_id={"dp": dp + 1 - 2 * core}, device_id_type=MESH_ID)
+    for step in range(1, seq_parts):
+        pl.semaphore_signal(barrier, inc=1, device_id={"seq": seq_of(step)}, device_id_type=MESH_ID)
+    for step in range(1, half_parts):
+        pl.semaphore_signal(
+            barrier, inc=1, device_id={"dp": line_of(step) * 2 + core}, device_id_type=MESH_ID
+        )
+    pl.semaphore_wait(barrier, seq_parts + half_parts - 1)
+
+    def ds(start, size, unit):
+        return pl.ds(pl.multiple_of(start, unit), size)
+
+    def core_copies(step):
+        part = seq_of(step + 1)
+        peer = {"dp": dp + 1 - 2 * core}
+        copies = []
+        for place in range(half_parts):
+            copies.append(
+                pltpu.make_async_remote_copy(
+                    src_ref=ge_ref.at[
+                        ds((2 * place + 1 - core) * e_rows, e_rows, 16), ds(part * e_cols, e_cols, 128)
+                    ],
+                    dst_ref=core_e.at[step, place],
+                    send_sem=core_send.at[step, place],
+                    recv_sem=core_recv.at[step, place],
+                    device_id=peer,
+                    device_id_type=MESH_ID,
+                )
+            )
+        copies.append(
+            pltpu.make_async_remote_copy(
+                src_ref=gp_ref.at[:, ds((2 * part + 1 - core) * p_cols, p_cols, 128)],
+                dst_ref=core_p.at[step],
+                send_sem=core_send.at[step, half_parts],
+                recv_sem=core_recv.at[step, half_parts],
+                device_id=peer,
+                device_id_type=MESH_ID,
+            )
+        )
+        return copies
+
+    def plane_e_copy(step):
+        return pltpu.make_async_remote_copy(
+            src_ref=core_e.at[step],
+            dst_ref=plane_e.at[step],
+            send_sem=es_send.at[step],
+            recv_sem=es_recv.at[step],
+            device_id={"seq": seq_of(step + 1)},
+            device_id_type=MESH_ID,
+        )
+
+    def plane_p_copy(step, hop):
+        part = seq_of(step + 1)
+        return pltpu.make_async_remote_copy(
+            src_ref=core_p.at[step, ds(seq_of(hop) * p_rows, p_rows, 16), :],
+            dst_ref=plane_p.at[part, hop - 1],
+            send_sem=ps_send.at[step, hop - 1],
+            recv_sem=ps_recv.at[part, hop - 1],
+            device_id={"seq": seq_of(hop)},
+            device_id_type=MESH_ID,
+        )
+
+    def line_e_copy(hop):
+        return pltpu.make_async_remote_copy(
+            src_ref=part_e.at[line_of(hop)],
+            dst_ref=line_e.at[hop - 1],
+            send_sem=ez_send.at[hop - 1],
+            recv_sem=ez_recv.at[hop - 1],
+            device_id={"dp": line_of(hop) * 2 + core},
+            device_id_type=MESH_ID,
+        )
+
+    def line_p_copy(hop):
+        return pltpu.make_async_remote_copy(
+            src_ref=part_p.at[line_of(hop)],
+            dst_ref=line_p.at[hop - 1],
+            send_sem=pz_send.at[hop - 1],
+            recv_sem=pz_recv.at[hop - 1],
+            device_id={"dp": line_of(hop) * 2 + core},
+            device_id_type=MESH_ID,
+        )
+
+    def add_core(step):
+        part = seq_of(step + 1)
+        for copy in core_copies(step):
+            copy.wait()
+        for place in range(half_parts):
+            own = ge_ref[ds((2 * place + core) * e_rows, e_rows, 16), ds(part * e_cols, e_cols, 128)]
+            core_e[step, place] = (own.astype(f32) + core_e[step, place].astype(f32)).astype(bf16)
+        own = gp_ref[:, ds((2 * part + core) * p_cols, p_cols, 128)]
+        core_p[step] = (own.astype(f32) + core_p[step].astype(f32)).astype(bf16)
+
+    def send_plane(step):
+        if step < seq_parts - 1:
+            plane_e_copy(step).start()
+        for hop in range(1, seq_parts):
+            plane_p_copy(step, hop).start()
+
+    def add_plane_p(step):
+        part = seq_of(step + 1)
+        total = core_p[step, ds(seq * p_rows, p_rows, 16), :].astype(f32)
+        for hop in range(1, seq_parts):
+            copy = plane_p_copy(step, hop)
+            copy.wait_send()
+            copy.wait_recv()
+            total = total + plane_p[part, hop - 1].astype(f32)
+        part_p[part] = total.astype(bf16)
+
+    def add_plane_e():
+        last = seq_parts - 1
+        for step in range(last):
+            copy = plane_e_copy(step)
+            copy.wait()
+        for place in range(half_parts):
+            total = core_e[last, place].astype(f32)
+            for step in range(last):
+                total = total + plane_e[step, place].astype(f32)
+            part_e[place] = total.astype(bf16)
+
+    ones_row = lax.broadcasted_iota(jnp.int32, (16, stretch), 0) == 0
+    qaug[HD : HD + 16, :] = jnp.where(ones_row, 1.0, 0.0).astype(bf16)
+    qaug[HD + 16 :, :] = jnp.zeros((HD - 16, stretch), bf16)
+    pair[...] = jnp.zeros(pair.shape, bf16)
+    dkv_ref[...] = jnp.zeros(dkv_ref.shape, f32)
+    for step in range(seq_parts):
+        for copy in core_copies(step):
+            copy.start()
+    key_pos = lax.broadcasted_iota(jnp.int32, (stretch, stretch), 0)
+    query_pos = lax.broadcasted_iota(jnp.int32, (stretch, stretch), 1)
+
+    def one_head(head, carry):
+        for step in range(seq_parts):
+            @pl.when(head == 1 + 2 * step)
+            def _(step=step):
+                add_core(step)
+
+            @pl.when(head == 2 + 2 * step)
+            def _(step=step):
+                send_plane(step)
+
+        rows = ds(head * HD, HD, HD)
+        query = q_ref[rows, :]
+        qaug[0:HD, :] = query
+        top = None
+        for block in range(blocks):
+            span = slice(block * stretch, (block + 1) * stretch)
+            part = jnp.dot(kaug_ref[span, :], qaug[...], preferred_element_type=f32)
+            if block == 0:
+                part = jnp.where(key_pos <= query_pos, part, masked_score)
+            score[span, :] = part
+            block_top = jnp.max(part, axis=0, keepdims=True)
+            top = block_top if top is None else jnp.maximum(top, block_top)
+        total = jnp.zeros((1, stretch), f32)
+        mixed = jnp.zeros((HD, stretch), f32)
+        for block in range(blocks):
+            span = slice(block * stretch, (block + 1) * stretch)
+            raised = jnp.exp(score[span, :] - top)
+            total = total + jnp.sum(raised, axis=0, keepdims=True)
+            low = raised.astype(bf16)
+            expo[span, :] = low
+            mixed = mixed + jnp.dot(kvt_ref[HD:, span], low, preferred_element_type=f32)
+        scale = 1.0 / total
+        mixed = mixed * scale
+        mix_ref[rows, :] = mixed.astype(bf16)
+        grad = gm_ref[rows, :].astype(f32) * scale
+        delta = jnp.sum(grad * mixed, axis=0, keepdims=True)
+        grad = grad.astype(bf16)
+        pair[0:HD, 0:stretch] = query
+        pair[HD:, stretch:] = grad
+        grad_query = jnp.zeros((HD, stretch), f32)
+        for block in range(blocks):
+            span = slice(block * stretch, (block + 1) * stretch)
+            part = jnp.dot(val_ref[span, :], grad, preferred_element_type=f32)
+            low = expo[span, :]
+            grad_score = (low.astype(f32) * (part - delta)).astype(bf16)
+            grad_query = grad_query + jnp.dot(
+                kvt_ref[0:HD, span], grad_score, preferred_element_type=f32
+            )
+            dkv_ref[span, :] += lax.dot_general(
+                jnp.concatenate([grad_score, low], axis=1), pair[...], NT_DIMS,
+                preferred_element_type=f32,
+            )
+        dq_ref[rows, :] = grad_query
+        return carry
+
+    lax.fori_loop(0, HEADS, one_head, 0)
+    for step in range(seq_parts):
+        add_plane_p(step)
+    add_plane_e()
+    for hop in range(1, half_parts):
+        line_e_copy(hop).start()
+        line_p_copy(hop).start()
+    total_e = part_e[line].astype(f32)
+    total_p = part_p[line].astype(f32)
+    for hop in range(1, half_parts):
+        line_e_copy(hop).wait()
+        line_p_copy(hop).wait()
+        total_e = total_e + line_e[hop - 1].astype(f32)
+        total_p = total_p + line_p[hop - 1].astype(f32)
+    oute_ref[...] = total_e
+    outp_ref[...] = total_p
+
+
+def attend_and_reduce(seq_parts, dp_parts, query_t, grad_t, kaug, values, kvt, grad_e, grad_p):
+    half = dp_parts // 2
+    width, stretch = query_t.shape
+    whole_len = kaug.shape[0]
+    e_rows, e_cols = grad_e.shape[0] // dp_parts, grad_e.shape[1] // seq_parts
+    p_rows, p_cols = grad_p.shape[0] // seq_parts, grad_p.shape[1] // dp_parts
+    dma = pltpu.SemaphoreType.DMA
+    vm = pl.BlockSpec(memory_space=pltpu.VMEM)
+    return pl.pallas_call(
+        functools.partial(attend_kernel, seq_parts, half),
+        out_shape=(
+            jax.ShapeDtypeStruct((width, stretch), bf16),
+            jax.ShapeDtypeStruct((width, stretch), f32),
+            jax.ShapeDtypeStruct((whole_len, 2 * HD), f32),
+            jax.ShapeDtypeStruct((e_rows, e_cols), f32),
+            jax.ShapeDtypeStruct((p_rows, p_cols), f32),
+        ),
+        in_specs=[vm] * 7,
+        out_specs=(vm,) * 5,
+        scratch_shapes=[
+            pltpu.VMEM((whole_len, stretch), f32),
+            pltpu.VMEM((whole_len, stretch), bf16),
+            pltpu.VMEM((2 * HD, stretch), bf16),
+            pltpu.VMEM((2 * HD, 2 * stretch), bf16),
+            pltpu.VMEM((seq_parts, half, e_rows, e_cols), bf16),
+            pltpu.VMEM((seq_parts, grad_p.shape[0], p_cols), bf16),
+            pltpu.VMEM((seq_parts - 1, half, e_rows, e_cols), bf16),
+            pltpu.VMEM((seq_parts, seq_parts - 1, p_rows, p_cols), bf16),
+            pltpu.VMEM((half, e_rows, e_cols), bf16),
+            pltpu.VMEM((half, p_rows, p_cols), bf16),
+            pltpu.VMEM((half - 1, e_rows, e_cols), bf16),
+            pltpu.VMEM((half - 1, p_rows, p_cols), bf16),
+            dma((seq_parts, half + 1)), dma((seq_parts, half + 1)),
+            dma((seq_parts - 1,)), dma((seq_parts - 1,)),
+            dma((seq_parts, seq_parts - 1)), dma((seq_parts, seq_parts - 1)),
+            dma((half - 1,)), dma((half - 1,)),
+            dma((half - 1,)), dma((half - 1,)),
+        ],
+        compiler_params=pltpu.CompilerParams(
+            collective_id=0, has_side_effects=True, vmem_limit_bytes=60 << 20
+        ),
+        cost_estimate=pl.CostEstimate(
+            flops=24 * width * stretch * whole_len, bytes_accessed=20 << 20, transcendentals=0
+        ),
+    )(query_t, grad_t, kaug, values, kvt, grad_e, grad_p)
+
+
+def fast_device(
+    hidden_in, seq_lengths, attention_gain, attention_shift, feed_gain, feed_shift, query_weight,
+    query_bias, keyval_weight, keyval_bias, dense_weight, dense_bias, expand_weight, expand_bias,
+    project_weight, project_bias, out_grad,
+):
+    _, stretch, width = hidden_in.shape
+    seq_parts = lax.axis_size("seq")
+    dp_parts = lax.axis_size("dp")
+    whole_len = stretch * seq_parts
+    seq = lax.axis_index("seq")
+    positions = seq * stretch + jnp.arange(stretch, dtype=jnp.int32)
+    query_scale = HD ** (-0.5)
+    inputs = hidden_in[0].astype(f32)
+    length = seq_lengths[0]
+    grad_out = jnp.where((positions < length)[:, None], out_grad[0], jnp.zeros_like(out_grad[0]))
+    attn_norm, attn_norm_back = jax.vjp(layer_norm, inputs, attention_gain, attention_shift)
+    feed_norm, feed_norm_back = jax.vjp(layer_norm, inputs, feed_gain, feed_shift)
+    attn_in = attn_norm.astype(bf16)
+    feed_in = feed_norm.astype(bf16)
+
+    def turn_query(flat_query):
+        shaped = flat_query.reshape(stretch, HEADS, HD).transpose(1, 0, 2)
+        return rotate(shaped, positions) * query_scale
+
+    def turn_keyval(flat_keyval):
+        return jnp.concatenate([rotate(flat_keyval[:, :HD], positions), flat_keyval[:, HD:]], axis=-1)
+
+    keyval_pre = jnp.dot(attn_in, keyval_weight, preferred_element_type=f32) + keyval_bias
+    keyval_rot, keyval_back = jax.vjp(turn_keyval, keyval_pre)
+    gathered = lax.all_gather(keyval_rot.astype(bf16), "seq", axis=0, tiled=True)
+    query_pre = jnp.dot(attn_in, query_weight, preferred_element_type=f32) + query_bias
+    query_rot, query_back = jax.vjp(turn_query, query_pre)
+    query_t = query_rot.astype(bf16).transpose(0, 2, 1).reshape(width, stretch)
+    grad_mixed_t = lax.dot_general(
+        dense_weight, grad_out, NT_DIMS, preferred_element_type=f32
+    ).astype(bf16)
+    upper = jnp.dot(feed_in, expand_weight, preferred_element_type=f32) + expand_bias
+    active, active_back = jax.vjp(exact_gelu, upper)
+    active_low = active.astype(bf16)
+    feed_out = jnp.dot(active_low, project_weight, preferred_element_type=f32) + project_bias
+    grad_active = jnp.dot(grad_out, project_weight.T, preferred_element_type=f32)
+    grad_upper = active_back(grad_active)[0].astype(bf16)
+    grad_feed_in = jnp.dot(grad_upper, expand_weight.T, preferred_element_type=f32)
+    feed_dx, feed_dgain, feed_dshift = feed_norm_back(grad_feed_in)
+    expand_term = outer_sum(feed_in, grad_upper).astype(bf16)
+    project_term = outer_sum(grad_out, active_low).astype(bf16)
+
+    rolled = jnp.roll(gathered.reshape(seq_parts, stretch, 2 * HD), -seq, axis=0)
+    block_seq = lax.rem(seq + jnp.arange(seq_parts, dtype=jnp.int32), seq_parts)
+    key_pos = block_seq[:, None] * stretch + jnp.arange(stretch, dtype=jnp.int32)[None, :]
+    usable = (block_seq <= seq)[:, None] & (key_pos < length)
+    rolled = rolled.reshape(whole_len, 2 * HD)
+    fence = jnp.where(usable.reshape(whole_len, 1), 0.0, masked_score).astype(bf16)
+    kaug = jnp.concatenate(
+        [rolled[:, :HD], fence, jnp.zeros((whole_len, HD - 1), bf16)], axis=1
+    )
+    mixed_t, grad_query_t, grad_keyval, expand_grad, project_grad = attend_and_reduce(
+        seq_parts, dp_parts, query_t, grad_mixed_t, kaug, rolled[:, HD:], rolled.T,
+        expand_term, project_term,
+    )
+    grad_keyval = jnp.roll(grad_keyval.reshape(seq_parts, stretch, 2 * HD), seq, axis=0)
+    grad_keyval_own = lax.psum_scatter(
+        grad_keyval.reshape(whole_len, 2 * HD), "seq", scatter_dimension=0, tiled=True
+    )
+    attn_out = lax.dot_general(
+        mixed_t, dense_weight, (((0,), (0,)), ((), ())), preferred_element_type=f32
+    ) + dense_bias
+    output = (inputs + attn_out + feed_out).astype(bf16)[None]
+    grad_query_all = grad_query_t.reshape(HEADS, HD, stretch).transpose(0, 2, 1)
+    grad_query_pre = query_back(grad_query_all)[0].astype(bf16)
+    grad_keyval_pre = keyval_back(grad_keyval_own)[0].astype(bf16)
+    grad_attn_in = jnp.dot(grad_query_pre, query_weight.T, preferred_element_type=f32) + jnp.dot(
+        grad_keyval_pre, keyval_weight.T, preferred_element_type=f32
+    )
+    attn_dx, attn_dgain, attn_dshift = attn_norm_back(grad_attn_in)
+    input_grad = (grad_out.astype(f32) + attn_dx + feed_dx)[None]
+    terms = (
+        outer_sum(attn_in, grad_query_pre),
+        outer_sum(attn_in, grad_keyval_pre),
+        jnp.dot(mixed_t, grad_out, preferred_element_type=f32),
+    )
+    row_sums = [lax.psum_scatter(v, "dp", scatter_dimension=0, tiled=True) for v in terms]
+    grads = [lax.psum_scatter(v, "seq", scatter_dimension=1, tiled=True) for v in row_sums]
+    small = lax.psum(
+        (
+            attn_dgain, attn_dshift, feed_dgain, feed_dshift,
+            jnp.sum(grad_query_pre, axis=0, dtype=f32),
+            jnp.sum(grad_keyval_pre, axis=0, dtype=f32),
+            jnp.sum(grad_out, axis=0, dtype=f32),
+            jnp.sum(grad_upper, axis=0, dtype=f32),
+        ),
+        ("seq", "dp"),
+    )
+    return (
+        output, input_grad, small[0], small[1], small[2], small[3], grads[0], small[4], grads[1],
+        small[5], grads[2], small[6], expand_grad, small[7], project_grad.T, small[6],
+    )
+
+
+def fits(hidden, expand_weight):
+    seq_parts, dp_parts = lax.axis_size("seq"), lax.axis_size("dp")
+    width, hidden_units = expand_weight.shape
+    return (
+        hidden.shape[0] == 1
+        and dp_parts == 2 * seq_parts
+        and width % (16 * dp_parts) == 0
+        and width % (16 * seq_parts) == 0
+        and hidden_units % (128 * dp_parts) == 0
+        and hidden.shape[1] % 128 == 0
+    )
+
+
 def solution(mesh):
+    def either_way(*args):
+        return (fast_device if fits(args[0], args[12]) else per_device)(*args)
+
     return jax.shard_map(
-        per_device,
+        either_way,
         mesh=mesh,
         in_specs=(
             P("dp", "seq", None),

time: 717 us -> 416 us (0.58)
  waiting for transfers between devices: 344 us -> 128 us
  matrix products: 185 us -> 73.3 us
  Pallas kernels: 0 us -> 93.7 us
  other arithmetic: 87.4 us -> 23.7 us
    reduce_scatter x7 -> x4, waiting for transfers between devices: 292 us -> 96.4 us  [the longest x3 77.2 us: fast_device(): lax.psum_scatter(v, 'dp', scatter_dimension=0, tiled=True)]
    dot_general x28 -> x11, matrix products: 164 us -> 59.1 us  [the longest x1 19.6 us: fast_device(): jnp.dot(feed_in, expand_weight, preferred_element_type=f32) + expand_bias]
    pallas_call x0 -> x1, Pallas kernels: none -> 93.7 us  [attend_and_reduce(): pl.pallas_call(functools.partial(attend_kernel, seq_parts, half), out_sha...]
    convert_element_type x4 -> x3, other arithmetic: 49.5 us -> 2.73 us  [the longest x1 2.37 us: fast_device(): query_t = query_rot.astype(bf16).transpose(0, 2, 1).reshape(width, stretch)]
    unnamed x15 -> x10, waiting for transfers between devices: 51.7 us -> 31.9 us
    reduce_sum x7 -> x3, other arithmetic: 20.5 us -> 4.51 us  [the longest x1 4.2 us: fast_device(): jnp.sum(grad_out, axis=0, dtype=f32)]
    dot_general x5 -> x4, matrix products: 21.3 us -> 14.2 us  [outer_sum(): lax.dot_general(left, right, (((0,), (0,)), ((), ())), preferred_element_...]
    unnamed x85 -> x112, local copies, waits for them, and re-layouts: 15.7 us -> 18.9 us
  transfers between devices with their start and end apart: 11 -> 7, of which waited for: 8 -> 6; matrix products, arithmetic and copies ran while one was open for 13% -> 13% of each run, Pallas kernels for 0% -> 0%
where the time goes in v1:
time: 416 us; the launch traced here: 415 us
  waiting for transfers between devices  128 us (31%)
  Pallas kernels  93.7 us (23%)
  matrix products  73.3 us (18%)
  blocking collectives  51 us (12%)
  local copies, waits for them, and re-layouts  29.1 us (7%)
  other arithmetic  23.7 us (6%)
  between operations  15.5 us (4%)
    pallas_call x1, Pallas kernels, attend_and_reduce(): pl.pallas_call(functools.partial(attend_kernel, seq_parts, half), out_sha...  93.7 us
    reduce_scatter x3, waiting for transfers between devices, fast_device(): lax.psum_scatter(v, 'dp', scatter_dimension=0, tiled=True)  77.2 us
    psum x1, blocking collectives, fast_device(): lax.psum((attn_dgain, attn_dshift, feed_dgain, feed_dshift, jnp.sum(grad_...  39.5 us
    unnamed x10, waiting for transfers between devices  31.9 us
    dot_general x1, matrix products, fast_device(): jnp.dot(feed_in, expand_weight, preferred_element_type=f32) + expand_bias  19.6 us
    reduce_scatter x1, waiting for transfers between devices, fast_device(): lax.psum_scatter(grad_keyval.reshape(whole_len, 2 * HD), 'seq', scatter_d...  19.3 us
    unnamed x112, local copies, waits for them, and re-layouts  18.9 us
    dot_general x4, matrix products, outer_sum(): lax.dot_general(left, right, (((0,), (0,)), ((), ())), preferred_element_...  14.2 us
  transfers between devices with their start and end apart: 7, of which 6 were waited for; matrix products, arithmetic and copies ran while one was open for 13% of the time, Pallas kernels for 0%

profile of v1, /device:TPU:0, one launch (start us, length us, event | category | flops | bytes accessed | tf_op | source)
XLA Modules:
  0.0 415.2 jit_solution(5838024212431883682)
XLA Ops:
  8.7 1.3 convert_reduce_fusion.1
  10.1 1.5 fusion.26
  14.4 11.5 %all_gather.3 = bf16[2048,128]{0,1:T(8,128)(2,1)S(1)} all-gather(bf16[512,128]{0,1:T(8,128)(2,1)S(1)} %pad_maximum_fusion), channel_id=1, replica_groups=mesh['seq'=4,'dp'=8] {'seq'}, dimensions={0}, use_global_device_ids=true | all-gather | bytes 655360 | tf_op jit(solution)/shard_map/all_gather | solution.py:551
  25.9 1.2 reshape.274
  27.1 2.2 fusion.46
  30.3 1.0 copy.48.val_ref
  32.2 1.0 copy.47.kaug_ref
  33.2 2.6 convolution_add_fusion.1
  35.8 1.9 copy.45
  37.8 1.2 slice.44
  39.7 1.8 fusion.37.gm_ref
  41.5 19.6 %multiply_convert_fusion = (bf16[512,3072]{1,0:T(8,128)(2,1)S(1)}, f32[512,3072]{1,0:T(8,128)}, f32[512,3072]{1,0:T(8,128)}) fusion(f32[3072]{0:T(1024)S(1)} %copy-done.43, bf16[768,3072]{1,0:T(8,128)(2,1)} %param.29, bf16[1,512,768]{2,1,0:T(8,128)(2,1)S(1)} %copy-done.1, f32[768]{0:T(1024)S(1)} %copy-done.44, f32[768]{0:T(1024)S(1)} %copy-done.24, ...), kind=kOutput, calls=%fused_computation.3 | convolution fusion | flops 2522087424 | bytes 21256192 | tf_op jit(solution)/shard_map/dot_general | solution.py:558
  61.2 9.1 %convert_reduce_fusion = (f32[3072]{0:T(1024)}, bf16[512,3072]{1,0:T(8,128)(2,1)S(1)}) fusion(f32[512,3072]{1,0:T(8,128)} %get-tuple-element.95, bf16[3072,768]{1,0:T(8,128)(2,1)S(1)} %bitcast.168, bf16[1,512,768]{2,1,0:T(8,128)(2,1)S(1)} %copy-done.3, pred[512]{0:T(512)(128)(4,1)S(1)} %copy-done.37, f32[512,3072]{1,0:T(8,128)} %get-tuple-element.114, ...), kind=kOutput, calls=%fused_computation.2 | convolution fusion | flops 2443047936 | bytes 21258752 | tf_op jit(solution)/shard_map/dot_general | solution.py:562
  70.3 4.8 %convolution_convert_fusion.1.ge_ref = bf16[768,3072]{1,0:T(8,128)(2,1)} fusion(bf16[512,3072]{1,0:T(8,128)(2,1)S(1)} %get-tuple-element.117, bf16[1,512,768]{2,1,0:T(8,128)(2,1)S(1)} %copy-done.1, f32[768]{0:T(1024)S(1)} %copy-done.44, f32[768]{0:T(1024)S(1)} %copy-done.24, f32[512]{0:T(512)S(1)} %copy-done.27, f32[512]{0:T(512)S(1)} %copy-done.18), kind=kOutput, calls=%fused_computation.19 | convolution fusion | flops 2420637696 | bytes 8660992 | tf_op jit(solution)/shard_map/dot_general | solution.py:52
  75.1 4.6 %convolution_convert_fusion.gp_ref = bf16[768,3072]{1,0:T(8,128)(2,1)} fusion(bf16[512,3072]{1,0:T(8,128)(2,1)S(1)} %get-tuple-element.94, bf16[1,512,768]{2,1,0:T(8,128)(2,1)S(1)} %copy-done.3, pred[512]{0:T(512)(128)(4,1)S(1)} %copy-done.37), kind=kOutput, calls=%fused_computation.18 | convolution fusion | flops 2418671616 | bytes 8651264 | tf_op jit(solution)/shard_map/dot_general | solution.py:52
  80.4 2.4 fusion.35
  82.8 93.7 %shard_map.288 = (bf16[768,512]{1,0:T(8,128)(2,1)}, f32[768,512]{1,0:T(8,128)}, f32[2048,128]{1,0:T(8,128)}, f32[96,768]{1,0:T(8,128)}, f32[192,384]{1,0:T(8,128)}) custom-call(bf16[768,512]{1,0:T(8,128)(2,1)} %bitcast.161, bf16[768,512]{1,0:T(8,128)(2,1)} %fusion.37.gm_ref, bf16[2048,128]{1,0:T(8,128)(2,1)} %copy.47.kaug_ref, ...), custom_call_target="tpu_custom_call" | custom-call | flops 19327352832 | bytes 20971520 | tf_op jit(solution)/shard_map/pallas_call | solution.py:483
  176.5 1.4 fusion.38
  177.8 1.3 copy.52
  179.2 1.6 broadcast_multiply_fusion
  182.7 2.5 fusion.40
  185.3 1.1 copy-done.4
  186.6 2.3 fusion.74
  189.0 5.9 %fusion.81 = f32[512,768]{1,0:T(8,128)S(1)} fusion(bf16[512,3072]{1,0:T(8,128)(2,1)} %copy-done.48, bf16[768,3072]{1,0:T(8,128)(2,1)} %param.29), kind=kOutput, calls=%fused_computation.138 | convolution fusion | flops 2415919104 | bytes 9437184 | tf_op jit(solution)/shard_map/dot_general | solution.py:564
  195.0 19.3 %reduce-scatter.14.cloned.1.call-done = f32[512,128]{0,1:T(8,128)} async-done(((f32[2048,128]{0,1:T(8,128)}), f32[512,128]{0,1:T(8,128)}) %reduce-scatter.14.cloned.1.call-update) | async-done | bytes 262160 | tf_op jit(solution)/shard_map/reduce_scatter | solution.py:583
  214.2 0.9 split.33
  215.1 0.9 split.32
  216.1 0.9 fusion.59
  217.7 2.3 fusion.67
  220.4 7.3 %fusion.80 = f32[512,768]{1,0:T(8,128)} fusion(bf16[512,3072]{1,0:T(8,128)(2,1)} %copy-done.47, bf16[3072,768]{1,0:T(8,128)(2,1)} %param.31), kind=kOutput, calls=%fused_computation.137 | convolution fusion | flops 2415919104 | bytes 9437184 | tf_op jit(solution)/shard_map/dot_general | solution.py:561
  228.3 3.9 fusion.36
  232.2 1.5 fusion.68
  233.8 19.9 %reduce-scatter.16.cloned.1.call-done = f32[96,768]{1,0:T(8,128)} async-done(((f32[768,768]{1,0:T(8,128)}), f32[96,768]{1,0:T(8,128)}) %reduce-scatter.16.cloned.1.call-update) | async-done | bytes 294928 | tf_op jit(solution)/shard_map/reduce_scatter | solution.py:603
  253.6 1.9 copy.53
  255.6 4.7 %fusion.77 = (f32[768]{0:T(1024)}, f32[512]{0:T(512)S(1)}, f32[512]{0:T(512)S(1)}, f32[768]{0:T(1024)}, f32[512,768]{1,0:T(8,128)}) fusion(f32[768]{0:T(1024)S(1)} %copy-done.23, f32[512]{0:T(512)S(1)} %copy-done.20, bf16[1,512,768]{2,1,0:T(8,128)(2,1)S(1)} %copy-done.1, f32[512,768]{1,0:T(8,128)S(1)} %fusion.81, f32[768]{0:T(1024)S(1)} %copy-done.25, ...), kind=kOutput, calls=%fused_computation.135 | convolution fusion | flops 608302592 | bytes 7489536 | tf_op jit(solution)/shard_map/dot_general | solution.py:593
  260.9 30.9 %reduce-scatter.20.cloned.1.call-done = f32[96,768]{1,0:T(8,128)} async-done(((f32[768,768]{1,0:T(8,128)}), f32[96,768]{1,0:T(8,128)}) %reduce-scatter.20.cloned.1.call-update) | async-done | bytes 294928 | tf_op jit(solution)/shard_map/reduce_scatter | solution.py:603
  291.8 1.9 copy.57
  293.8 3.2 fusion.25
  297.6 26.3 %reduce-scatter.18.cloned.1.call-done = f32[96,128]{1,0:T(8,128)} async-done(((f32[768,128]{1,0:T(8,128)}), f32[96,128]{1,0:T(8,128)}) %reduce-scatter.18.cloned.1.call-update) | async-done | bytes 49168 | tf_op jit(solution)/shard_map/reduce_scatter | solution.py:603
  324.0 1.5 copy.55
  325.5 4.2 %convert_reduce_fusion.2 = (f32[768]{0:T(1024)}, f32[1,512,768]{2,1,0:T(8,128)}) fusion(bf16[1,512,768]{2,1,0:T(8,128)(2,1)} %param.33, pred[512]{0:T(512)(128)(4,1)} %fusion.63, f32[512]{0:T(512)} %get-tuple-element.118, f32[512]{0:T(512)} %get-tuple-element.113, f32[512,768]{1,0:T(8,128)S(1)} %fusion.81, f32[768]{0:T(1024)S(1)} %copy-done.25, ...), kind=kLoop, calls=%fused_computation.39 | loop fusion | flops 7470336 | bytes 6313472 | tf_op jit(solution)/shard_map/reduce_sum | solution.py:610
  329.8 39.5 %all-reduce.8 = (f32[768]{0:T(1024)}, f32[768]{0:T(1024)}, f32[768]{0:T(1024)}, f32[768]{0:T(1024)}, f32[768]{0:T(1024)}, /*index=5*/f32[128]{0:T(128)}, f32[768]{0:T(1024)S(1)}, f32[3072]{0:T(1024)}) all-reduce(f32[768]{0:T(1024)} %get-tuple-element.83, f32[768]{0:T(1024)} %get-tuple-element.80, ...), channel_id=1, replica_groups=mesh['seq'=4,'dp'=8] {'seq','dp'}, use_global_device_ids=true, to_apply=%region_8.9 | all-reduce | flops 7808 | bytes 62464 | tf_op jit(solution)/shard_map/psum | solution.py:605
  369.4 1.6 copy.54
  371.0 6.0 %reduce-scatter.26.cloned.1.call-done = f32[192,96]{1,0:T(8,128)} async-done(((f32[768,96]{1,0:T(8,128)}), f32[192,96]{1,0:T(8,128)}) %reduce-scatter.26.cloned.1.call-update) | async-done | bytes 73744
  376.9 1.6 copy.58
  378.6 25.8 %reduce-scatter.24.cloned.1.call-done = f32[32,96]{1,0:T(8,128)} async-done(((f32[128,96]{1,0:T(8,128)}), f32[32,96]{1,0:T(8,128)}) %reduce-scatter.24.cloned.1.call-update) | async-done | bytes 12304
  405.0 1.7 copy.66
  406.7 1.7 copy.67
  (146 shorter events, 12.8 us)
Async XLA Ops:
  7.2 26.0 %copy-start = (bf16[768,768]{1,0:T(8,128)(2,1)S(1)}, bf16[768,768]{1,0:T(8,128)(2,1)}, u32[]{:S(2)}) copy-start(bf16[768,768]{1,0:T(8,128)(2,1)} %param.23) | copy-start | bytes 3538948
  7.2 5.6 %copy-start.1 = (bf16[1,512,768]{2,1,0:T(8,128)(2,1)S(1)}, bf16[1,512,768]{2,1,0:T(8,128)(2,1)}, u32[]{:S(2)}) copy-start(bf16[1,512,768]{2,1,0:T(8,128)(2,1)} %param.17) | copy-start | bytes 2359300
  7.2 5.6 %copy-start.21 = (f32[768]{0:T(1024)S(1)}, f32[768]{0:T(1024)}, u32[]{:S(2)}) copy-start(f32[768]{0:T(1024)} %param.19) | copy-start | bytes 9220
  7.2 5.6 %copy-start.34 = (f32[768]{0:T(1024)S(1)}, f32[768]{0:T(1024)}, u32[]{:S(2)}) copy-start(f32[768]{0:T(1024)} %param.20) | copy-start | bytes 9220
  7.2 207.0 %reduce-scatter.14.cloned.1.call-start = ((), (), s32[]{:S(2)}) async-start(), calls=%async_computation.7 | async-start | bytes 1310720 | tf_op jit(solution)/shard_map/reduce_scatter | solution.py:583
  7.3 6.3 %copy-start.39 = (f32[8]{0:T(128)}, f32[8]{0:T(128)S(1)}, u32[]{:S(2)}) copy-start(f32[8]{0:T(128)S(1)} %multiply_power_fusion) | copy-start | bytes 100
  8.1 5.5 %copy-start.32 = (f32[512]{0:T(512)}, f32[512]{0:T(512)S(1)}, u32[]{:S(2)}) copy-start(f32[512]{0:T(512)S(1)} %fusion.64) | copy-start | bytes 6148
  8.7 4.4 %copy-start.14 = (bf16[768,128]{1,0:T(8,128)(2,1)S(1)}, bf16[768,128]{1,0:T(8,128)(2,1)}, u32[]{:S(2)}) copy-start(bf16[768,128]{1,0:T(8,128)(2,1)} %param.25) | copy-start | bytes 589828
  8.7 4.4 %copy-start.41 = (f32[128]{0:T(128)S(1)}, f32[128]{0:T(128)}, u32[]{:S(2)}) copy-start(f32[128]{0:T(128)} %param.26) | copy-start | bytes 1540
  10.1 3.5 copy-start.17
  11.6 2.8 copy-start.26
  13.2 20.1 %copy-start.2 = (bf16[512,768]{1,0:T(8,128)(2,1)}, bf16[512,768]{1,0:T(8,128)(2,1)S(1)}, u32[]{:S(2)}) copy-start(bf16[512,768]{1,0:T(8,128)(2,1)S(1)} %fusion.21) | copy-start | bytes 2359300
  37.7 1.2 copy-start.3
  37.7 1.2 copy-start.37
  37.7 1.9 copy-start.42
  37.8 3.7 copy-start.43
  37.8 3.7 copy-start.44
  39.7 1.8 copy-start.18
  39.7 1.8 copy-start.24
  39.7 1.8 copy-start.27
  39.7 21.5 %slice-start = ((s8[4718592]{0:T(1024)(128)(4,1)}), s8[4194304]{0:T(1024)(128)(4,1)S(1)}, s32[]{:S(2)}) async-start(s8[4718592]{0:T(1024)(128)(4,1)} %bitcast.167), calls=%async_computation.14 | async-start | bytes 8388608
  41.5 19.7 %slice-start.1 = ((s8[4718592]{0:T(1024)(128)(4,1)}), s8[524288]{0:T(1024)(128)(4,1)S(1)}, s32[]{:S(2)}) async-start(s8[4718592]{0:T(1024)(128)(4,1)} %bitcast.167), calls=%async_computation.15 | async-start | bytes 1048576
  61.1 13.9 %copy-start.47 = (bf16[512,3072]{1,0:T(8,128)(2,1)}, bf16[512,3072]{1,0:T(8,128)(2,1)S(1)}, u32[]{:S(2)}) copy-start(bf16[512,3072]{1,0:T(8,128)(2,1)S(1)} %get-tuple-element.94) | copy-start | bytes 9437188
  70.3 4.8 %copy-start.48 = (bf16[512,3072]{1,0:T(8,128)(2,1)}, bf16[512,3072]{1,0:T(8,128)(2,1)S(1)}, u32[]{:S(2)}) copy-start(bf16[512,3072]{1,0:T(8,128)(2,1)S(1)} %get-tuple-element.117) | copy-start | bytes 9437188
  179.2 74.5 %reduce-scatter.16.cloned.1.call-start = ((), (), s32[]{:S(2)}) async-start(), calls=%async_computation.8 | async-start | bytes 2654208 | tf_op jit(solution)/shard_map/reduce_scatter | solution.py:603
  181.5 1.2 copy-start.35
  185.2 1.4 copy-start.13
  185.2 1.4 copy-start.38
  185.3 106.6 %reduce-scatter.20.cloned.1.call-start = ((), (), s32[]{:S(2)}) async-start(), calls=%async_computation.10 | async-start | bytes 2654208 | tf_op jit(solution)/shard_map/reduce_scatter | solution.py:603
  189.0 27.1 %copy-start.33 = (f32[512]{0:T(512)S(1)}, f32[512]{0:T(512)}, u32[]{:S(2)}) copy-start(f32[512]{0:T(512)} %copy-done.32) | copy-start | bytes 6148
  189.0 27.1 %copy-start.40 = (f32[8]{0:T(128)S(1)}, f32[8]{0:T(128)}, u32[]{:S(2)}) copy-start(f32[8]{0:T(128)} %copy-done.39) | copy-start | bytes 100
  189.0 135.0 %reduce-scatter.18.cloned.1.call-start = ((), (), s32[]{:S(2)}) async-start(), calls=%async_computation.9 | async-start | bytes 442368 | tf_op jit(solution)/shard_map/reduce_scatter | solution.py:603
  220.0 8.3 %copy-start.45 = (f32[768]{0:T(1024)S(1)}, f32[768]{0:T(1024)}, u32[]{:S(2)}) copy-start(f32[768]{0:T(1024)} %param.32) | copy-start | bytes 9220
  220.0 8.2 %copy-start.46 = (f32[768]{0:T(1024)S(1)}, f32[768]{0:T(1024)}, u32[]{:S(2)}) copy-start(f32[768]{0:T(1024)} %param.28) | copy-start | bytes 9220
  220.1 149.3 %reduce-scatter.22.cloned.1.call-start = ((), (), s32[]{:S(2)}) async-start(), calls=%async_computation.11 | async-start | bytes 491520
  228.3 3.9 copy-start.8
  228.3 3.9 copy-start.11
  228.3 3.9 copy-start.15
  232.2 23.4 %copy-start.20 = (f32[512]{0:T(512)S(1)}, f32[512]{0:T(512)}, u32[]{:S(2)}) copy-start(f32[512]{0:T(512)} %copy-done.17) | copy-start | bytes 6148
  232.2 23.4 %copy-start.23 = (f32[768]{0:T(1024)S(1)}, f32[768]{0:T(1024)}, u32[]{:S(2)}) copy-start(f32[768]{0:T(1024)} %param.19) | copy-start | bytes 9220
  232.2 23.4 %copy-start.25 = (f32[768]{0:T(1024)S(1)}, f32[768]{0:T(1024)}, u32[]{:S(2)}) copy-start(f32[768]{0:T(1024)} %param.21) | copy-start | bytes 9220
  255.5 38.3 %copy-start.29 = (f32[512]{0:T(512)S(1)}, f32[512]{0:T(512)}, u32[]{:S(2)}) copy-start(f32[512]{0:T(512)} %copy-done.26) | copy-start | bytes 6148
  255.5 121.4 %reduce-scatter.26.cloned.1.call-start = ((), (), s32[]{:S(2)}) async-start(), calls=%async_computation.13 | async-start | bytes 491520
  255.6 4.7 %copy-start.31 = (f32[512]{0:T(512)S(1)}, f32[512]{0:T(512)}, u32[]{:S(2)}) copy-start(f32[512]{0:T(512)} %copy-done.30) | copy-start | bytes 6148
  293.7 110.6 %reduce-scatter.24.cloned.1.call-start = ((), (), s32[]{:S(2)}) async-start(), calls=%async_computation.12 | async-start | bytes 81920
  325.5 4.2 %copy-start.9 = (f32[512,64]{0,1:T(8,128)S(1)}, f32[512,64]{0,1:T(8,128)}, u32[]{:S(2)}) copy-start(f32[512,64]{0,1:T(8,128)} %copy-done.7) | copy-start | bytes 393220
  325.5 4.2 %copy-start.12 = (f32[512,64]{0,1:T(8,128)S(1)}, f32[512,64]{0,1:T(8,128)}, u32[]{:S(2)}) copy-start(f32[512,64]{0,1:T(8,128)} %copy-done.10) | copy-start | bytes 393220
  369.4 39.0 %copy-start.36 = (f32[768]{0:T(1024)}, f32[768]{0:T(1024)S(1)}, u32[]{:S(2)}) copy-start(f32[768]{0:T(1024)S(1)} %get-tuple-element.179) | copy-start | bytes 9220
  (10 other events, 9.3 us)
Sparse Core Ops, SparseCore 0:
  179.3 34.9 reduce-scatter.13
  216.6 37.0 reduce-scatter.15
  255.9 35.8 reduce-scatter.19
  293.9 29.9 reduce-scatter.17
  326.6 22.8 reduce-scatter.21
  352.1 24.7 reduce-scatter.25
  380.2 24.0 reduce-scatter.23

commit v2 on v0

--- a/solution.py
+++ b/solution.py
@@ -1,11 +1,17 @@
+import functools
+
 import jax
 import jax.numpy as jnp
 from jax import lax
+from jax.experimental import pallas as pl
+from jax.experimental.pallas import tpu as pltpu
 from jax.sharding import PartitionSpec as P
 
 HEADS = 12
 HD = 64
 ROT = 16
+f32 = jnp.float32
+bf16 = jnp.bfloat16
 
 
 norm_eps = 1e-05
@@ -236,9 +242,630 @@
     )
 
 
+NT_DIMS = (((1,), (1,)), ((), ()))
+MESH_ID = pl.DeviceIdType.MESH
+VMEM_BYTES = 67043328
+
+
+def dot(left, right):
+    return jnp.dot(left, right, preferred_element_type=f32)
+
+
+def dot_nt(left, right):
+    return lax.dot_general(left, right, NT_DIMS, preferred_element_type=f32)
+
+
+def aligned(start, size, unit):
+    return pl.ds(pl.multiple_of(start, unit), size)
+
+
+class Place:
+    def __init__(self, seq_parts, half):
+        self.seq_parts, self.half = seq_parts, half
+        self.seq = lax.axis_index("seq")
+        self.dp = lax.axis_index("dp")
+        self.core = lax.rem(self.dp, 2)
+        self.line = lax.div(self.dp, 2)
+        self.partner = {"dp": self.dp + 1 - 2 * self.core}
+
+    def seq_at(self, hop):
+        return lax.rem(self.seq + hop, self.seq_parts)
+
+    def line_at(self, hop):
+        return lax.rem(self.line + hop, self.half)
+
+    def plane_peer(self, hop):
+        return {"seq": self.seq_at(hop)}
+
+    def line_peer(self, hop):
+        return {"dp": self.line_at(hop) * 2 + self.core}
+
+
+def remote(src, dst, send, recv, peer):
+    return pltpu.make_async_remote_copy(
+        src_ref=src, dst_ref=dst, send_sem=send, recv_sem=recv, device_id=peer,
+        device_id_type=MESH_ID,
+    )
+
+
+class Reduction:
+    def __init__(self, place, bufs, sems):
+        self.at = place
+        (self.ge, self.gp, self.ce, self.cp, self.pe, self.pp, self.te, self.tp, self.le,
+         self.lp) = bufs
+        (self.cs, self.cr, self.es, self.er, self.ps, self.pr, self.zs, self.zr) = sems
+
+    def core_copies(self, step):
+        at, slot = self.at, lax.rem(step, 2)
+        return [
+            remote(src.at[slot, 1 - at.core], dst.at[step], self.cs.at[step, i], self.cr.at[step, i],
+                   at.partner)
+            for i, (src, dst) in enumerate(((self.ge, self.ce), (self.gp, self.cp)))
+        ]
+
+    def core_start(self, step):
+        for copy in self.core_copies(step):
+            copy.start()
+
+    def core_finish(self, step):
+        at, slot = self.at, lax.rem(step, 2)
+        for copy in self.core_copies(step):
+            copy.wait()
+        for src, dst in ((self.ge, self.ce), (self.gp, self.cp)):
+            for i in range(dst.shape[1]):
+                dst[step, i] = (src[slot, at.core, i].astype(f32) + dst[step, i].astype(f32)).astype(
+                    bf16
+                )
+
+    def col_copy(self, step):
+        return remote(self.ce.at[step], self.pe.at[step], self.es.at[step], self.er.at[step],
+                      self.at.plane_peer(step + 1))
+
+    def row_copy(self, step, hop):
+        at, part = self.at, self.at.seq_at(step + 1)
+        return remote(self.cp.at[step, at.seq_at(hop)], self.pp.at[part, hop - 1],
+                      self.ps.at[step, hop - 1], self.pr.at[part, hop - 1], at.plane_peer(hop))
+
+    def plane_start(self, step):
+        @pl.when(step < self.at.seq_parts - 1)
+        def _():
+            self.col_copy(step).start()
+
+        for hop in range(1, self.at.seq_parts):
+            self.row_copy(step, hop).start()
+
+    def col_finish(self):
+        last = self.at.seq_parts - 1
+        for step in range(last):
+            self.col_copy(step).wait()
+        for i in range(self.at.half):
+            total = self.ce[last, i].astype(f32)
+            for step in range(last):
+                total = total + self.pe[step, i].astype(f32)
+            self.te[i] = total.astype(bf16)
+
+    def row_finish(self, step):
+        at, part = self.at, self.at.seq_at(step + 1)
+        total = self.cp[step, at.seq].astype(f32)
+        for hop in range(1, at.seq_parts):
+            self.row_copy(step, hop).wait()
+            total = total + self.pp[part, hop - 1].astype(f32)
+        self.tp[part] = total.astype(bf16)
+
+    def line_copy(self, family, hop):
+        at = self.at
+        src, dst = ((self.te, self.le), (self.tp, self.lp))[family]
+        return remote(src.at[at.line_at(hop)], dst.at[hop - 1], self.zs.at[family, hop - 1],
+                      self.zr.at[family, hop - 1], at.line_peer(hop))
+
+    def line_start(self, family):
+        for hop in range(1, self.at.half):
+            self.line_copy(family, hop).start()
+
+    def line_finish(self, family):
+        src, dst = ((self.te, self.le), (self.tp, self.lp))[family]
+        total = src[self.at.line].astype(f32)
+        for hop in range(1, self.at.half):
+            self.line_copy(family, hop).wait()
+            total = total + dst[hop - 1].astype(f32)
+        return total
+
+
+def reduction_scratch(seq_parts, half, col_block, row_block):
+    dma = pltpu.SemaphoreType.DMA
+    hops, legs = seq_parts - 1, half - 1
+    bufs = [
+        (2, 2, half) + col_block, (2, 2, seq_parts) + row_block,
+        (seq_parts, half) + col_block, (seq_parts, seq_parts) + row_block,
+        (hops, half) + col_block, (seq_parts, hops) + row_block,
+        (half,) + col_block, (half,) + row_block,
+        (legs,) + col_block, (legs,) + row_block,
+    ]
+    sems = [
+        dma((seq_parts, 2)), dma((seq_parts, 2)), dma((hops,)), dma((hops,)),
+        dma((seq_parts, hops)), dma((seq_parts, hops)), dma((2, legs)), dma((2, legs)),
+    ]
+    return [pltpu.VMEM(shape, bf16) for shape in bufs] + sems
+
+
+class Small:
+    def __init__(self, place, cbuf, pbuf, zbuf, sems):
+        self.at, self.cbuf, self.pbuf, self.zbuf = place, cbuf, pbuf, zbuf
+        self.cs, self.cr, self.ps, self.pr, self.zs, self.zr = sems
+
+    def core_copy(self, src):
+        return remote(src, self.cbuf, self.cs.at[0], self.cr.at[0], self.at.partner)
+
+    def plane_copy(self, hop):
+        at = self.at
+        mine = self.pbuf.at[at.seq]
+        return remote(mine, mine, self.ps.at[hop - 1], self.pr.at[hop - 1], at.plane_peer(hop))
+
+    def plane_start(self, value):
+        self.pbuf[self.at.seq] = value
+        for hop in range(1, self.at.seq_parts):
+            self.plane_copy(hop).start()
+
+    def plane_finish(self):
+        for hop in range(1, self.at.seq_parts):
+            self.plane_copy(hop).wait()
+        total = self.pbuf[0].astype(f32)
+        for i in range(1, self.at.seq_parts):
+            total = total + self.pbuf[i].astype(f32)
+        return total
+
+    def line_copy(self, hop, src=None):
+        at = self.at
+        mine = self.zbuf.at[at.line]
+        return remote(mine if src is None else src, mine, self.zs.at[hop - 1], self.zr.at[hop - 1],
+                      at.line_peer(hop))
+
+    def line_sum(self):
+        total = self.zbuf[0].astype(f32)
+        for i in range(1, self.at.half):
+            total = total + self.zbuf[i].astype(f32)
+        return total
+
+
+def layer_kernel(seq_parts, half, *refs):
+    refs = list(refs)
+
+    def take(count):
+        taken, refs[:count] = refs[:count], []
+        return taken
+
+    (length_ref, cos_ref, sin_ref, again_ref, ashift_ref, fgain_ref, fshift_ref, qbias_ref,
+     kvbias_ref, dbias_ref, ebias_ref, pbias_ref) = take(12)
+    hid_hbm, og_hbm, wq_hbm, wkv_hbm, wd_hbm, we_hbm, wp_hbm = take(7)
+    out_ref, dx_ref, eout_ref, pout_ref, qout_ref, dout_ref, kvout_ref, small_ref = take(8)
+    (hid, go, wq, wkv, wd, we, wp, norm, rstd, feed, feed_t, go_t, attn_t, base, query_t, gm_t, mix_t,
+     gq_t, kvt, kt, vt, kaug, kv, score, expo, qaug, pair, dkv, dkv_out, dkv_in, kvg, small_own,
+     kvz) = take(33)
+    load_sem, kv_send, kv_recv, dk_send, dk_recv = take(5)
+    place = Place(seq_parts, half)
+    feed_sum = Reduction(place, take(10), take(8))
+    attn_sum = Reduction(place, take(10), take(8))
+    vec_sum = Small(place, *take(3), take(6))
+    kvw_sum = Small(place, *take(3), take(6))
+    seq, core, line = place.seq, place.core, place.line
+    stretch, width = hid.shape
+    chunk = we.shape[2]
+    col_rows = feed_sum.ge.shape[3]
+    row_rows = feed_sum.gp.shape[3]
+    row_cols = feed_sum.gp.shape[4]
+    group = HEADS // seq_parts
+    group_rows = group * HD
+    half_rot = ROT // 2
+    scale = HD ** (-0.5)
+
+    def load(src, dst, index):
+        return pltpu.make_async_copy(src, dst, load_sem.at[index])
+
+    def load_chunk(step):
+        slot = lax.rem(step, 2)
+        start = place.seq_at(step + 1) * chunk
+        return (
+            load(we_hbm.at[:, aligned(start, chunk, 128)], we.at[slot], 5 + 2 * slot),
+            load(wp_hbm.at[aligned(start, chunk, 16), :], wp.at[slot], 6 + 2 * slot),
+        )
+
+    loads = (load(hid_hbm, hid, 0), load(wkv_hbm, wkv, 1), load(wq_hbm, wq, 2), load(og_hbm, go, 3),
+             load(wd_hbm, wd, 4))
+    for copy in loads:
+        copy.start()
+    for copy in load_chunk(0):
+        copy.start()
+
+    barrier = pltpu.get_barrier_semaphore()
+    pl.semaphore_signal(barrier, inc=1, device_id=place.partner, device_id_type=MESH_ID)
+    for hop in range(1, seq_parts):
+        pl.semaphore_signal(barrier, inc=1, device_id=place.plane_peer(hop), device_id_type=MESH_ID)
+    for hop in range(1, half):
+        pl.semaphore_signal(barrier, inc=1, device_id=place.line_peer(hop), device_id_type=MESH_ID)
+
+    length = length_ref[0]
+    loads[0].wait()
+    values = hid[...].astype(f32)
+    average = jnp.mean(values, axis=1, keepdims=True)
+    centered = values - average
+    inverse = lax.rsqrt(jnp.mean(centered * centered, axis=1, keepdims=True) + norm_eps)
+    normed = centered * inverse
+    norm[...] = normed
+    rstd[...] = jnp.broadcast_to(inverse, rstd.shape)
+    base[...] = values + (dbias_ref[...] + pbias_ref[...])
+    attn_t[...] = (normed * again_ref[...] + ashift_ref[...]).astype(bf16).T
+    low = (normed * fgain_ref[...] + fshift_ref[...]).astype(bf16)
+    feed[...] = low
+    feed_t[...] = low.T
+
+    def turn(rows, direction):
+        lead, pair_part = rows[0:half_rot, :], rows[half_rot:ROT, :]
+        cosine, sine = cos_ref[...], sin_ref[...] * direction
+        return jnp.concatenate(
+            [lead * cosine - pair_part * sine, pair_part * cosine + lead * sine, rows[ROT:, :]], axis=0
+        )
+
+    loads[1].wait()
+    own = lax.dot_general(wkv[...], attn_t[...], (((0,), (0,)), ((), ())),
+                          preferred_element_type=f32) + kvbias_ref[...]
+    kvt[0] = jnp.concatenate([turn(own[0:HD, :], 1.0), own[HD:, :]], axis=0).astype(bf16)
+
+    def kv_copy(hop):
+        return remote(kvt.at[0], kvt.at[seq_parts - hop], kv_send.at[hop - 1], kv_recv.at[hop - 1],
+                      place.plane_peer(hop))
+
+    pl.semaphore_wait(barrier, seq_parts + half - 1)
+    loads[2].wait()
+    wq_t = wq[...].T
+    for hop in range(1, seq_parts):
+        kv_copy(hop).start()
+    for head in range(HEADS):
+        span = slice(head * HD, (head + 1) * HD)
+        rows = dot(wq_t[span, :], attn_t[...]) + qbias_ref[span, :]
+        query_t[span, :] = (turn(rows, 1.0) * scale).astype(bf16)
+
+    loads[3].wait()
+    token = seq * stretch + lax.broadcasted_iota(jnp.int32, (stretch, 1), 0)
+    masked = jnp.where(token < length, go[...].astype(f32), 0.0).astype(bf16)
+    go[...] = masked
+    go_t[...] = masked.T
+    loads[4].wait()
+    gm_t[...] = dot(wd[...], go_t[...]).astype(bf16)
+    ones = jnp.ones((16, stretch), bf16)
+    small_own[...] = jnp.zeros(small_own.shape, f32)
+    parts = seq_parts
+    small_own[parts + 2 : parts + 3, :] = dot(ones, go[...])[0:1, :]
+
+    dx_ref[...] = jnp.zeros(dx_ref.shape, f32)
+
+    def feed_step(step, carry):
+        slot = lax.rem(step, 2)
+        part = place.seq_at(step + 1)
+
+        @pl.when(step + 1 < seq_parts)
+        def _():
+            for copy in load_chunk(step + 1):
+                copy.start()
+
+        for copy in load_chunk(step):
+            copy.wait()
+        upper = dot(feed[...], we[slot]) + ebias_ref[part]
+        grad_active = dot_nt(go[...], wp[slot])
+        share = 0.5 * (1.0 + lax.erf(upper * (0.5**0.5)))
+        slope = share + upper * (jnp.exp(-0.5 * upper * upper) * 0.3989422804014327)
+        active = (upper * share).astype(bf16)
+        grad_upper = (grad_active * slope).astype(bf16)
+        col_grad = dot(feed_t[...], grad_upper).astype(bf16)
+        for i in range(2 * half):
+            feed_sum.ge[slot, i % 2, i // 2] = col_grad[i * col_rows : (i + 1) * col_rows, :]
+        row_grad = dot(go_t[...], active).astype(bf16)
+        for c in range(2):
+            for i in range(seq_parts):
+                feed_sum.gp[slot, c, i] = row_grad[
+                    i * row_rows : (i + 1) * row_rows, c * row_cols : (c + 1) * row_cols
+                ]
+        small_own[pl.ds(part, 1), :] = dot(ones, grad_upper)[0:1, :]
+
+        @pl.when(step > 0)
+        def _():
+            feed_sum.core_finish(step - 1)
+
+        base[...] += dot(active, wp[slot])
+        dx_ref[...] += dot_nt(grad_upper, we[slot])
+
+        @pl.when(step > 0)
+        def _():
+            feed_sum.plane_start(step - 1)
+
+        feed_sum.core_start(step)
+        return carry
+
+    lax.fori_loop(0, seq_parts, feed_step, 0)
+    grad_feed = dx_ref[...]
+    small_own[parts : parts + 1, :] = jnp.sum(grad_feed * norm[...], axis=0, keepdims=True)
+    small_own[parts + 1 : parts + 2, :] = jnp.sum(grad_feed, axis=0, keepdims=True)
+    dx_ref[...] = grad_feed * fgain_ref[...]
+
+    lane = lax.broadcasted_iota(jnp.int32, (16, stretch), 1)
+    first = lax.broadcasted_iota(jnp.int32, (16, stretch), 0) == 0
+    unit_row = jnp.where(first, 1.0, 0.0).astype(bf16)
+    rest = jnp.zeros((HD - 16, stretch), bf16)
+    for hop in range(1, seq_parts):
+        kv_copy(hop).wait()
+    for i in range(seq_parts):
+        span = slice(i * stretch, (i + 1) * stretch)
+        held = kvt[i]
+        owner = place.seq_at(i)
+        usable = (owner * stretch + lane < length) & (owner <= seq)
+        fence = jnp.where(first & jnp.logical_not(usable), masked_score, 0.0).astype(bf16)
+        kaug[span, :] = jnp.concatenate([held[0:HD, :], fence, rest], axis=0).T
+        kv[span, :] = held.T
+        kt[:, span] = held[0:HD, :]
+        vt[0:HD, span] = held[HD:, :]
+        vt[HD:, span] = unit_row
+    qaug[HD : HD + 16, :] = unit_row
+    qaug[HD + 16 :, :] = rest
+    pair[...] = jnp.zeros(pair.shape, bf16)
+    dkv[...] = jnp.zeros(dkv.shape, f32)
+    key_pos = lax.broadcasted_iota(jnp.int32, (stretch, stretch), 0)
+    query_pos = lax.broadcasted_iota(jnp.int32, (stretch, stretch), 1)
+
+    def attend(head):
+        rows = aligned(head * HD, HD, HD)
+        query = query_t[rows, :]
+        qaug[0:HD, :] = query
+        top = None
+        for i in range(seq_parts):
+            span = slice(i * stretch, (i + 1) * stretch)
+            block = dot(kaug[span, :], qaug[...])
+            if i == 0:
+                block = jnp.where(key_pos <= query_pos, block, masked_score)
+            score[span, :] = block
+            block_top = jnp.max(block, axis=0, keepdims=True)
+            top = block_top if top is None else jnp.maximum(top, block_top)
+        mixed = jnp.zeros((HD + 16, stretch), f32)
+        for i in range(seq_parts):
+            span = slice(i * stretch, (i + 1) * stretch)
+            low = jnp.exp(score[span, :] - top).astype(bf16)
+            expo[span, :] = low
+            mixed = mixed + dot(vt[:, span], low)
+        inverse = 1.0 / mixed[HD : HD + 1, :]
+        mixed = mixed[0:HD, :] * inverse
+        mix_t[rows, :] = mixed.astype(bf16)
+        grad = (gm_t[rows, :].astype(f32) * inverse).astype(bf16)
+        delta = jnp.sum(grad.astype(f32) * mixed, axis=0, keepdims=True)
+        pair[0:HD, 0:stretch] = query
+        pair[HD:, stretch:] = grad
+        grad_query = jnp.zeros((HD, stretch), f32)
+        for i in range(seq_parts):
+            span = slice(i * stretch, (i + 1) * stretch)
+            block = dot(kv[span, :], pair[:, stretch:])
+            low = expo[span, :]
+            grad_score = (low.astype(f32) * (block - delta)).astype(bf16)
+            grad_query = grad_query + dot(kt[:, span], grad_score)
+            dkv[span, :] += dot_nt(jnp.concatenate([grad_score, low], axis=1), pair[...])
+        gq_t[rows, :] = (turn(grad_query, -1.0) * scale).astype(bf16)
+
+    def group_grads(step):
+        slot = lax.rem(step, 2)
+        rows = aligned(place.seq_at(step + 1) * group_rows, group_rows, 16)
+        col_grad = dot_nt(attn_t[...], gq_t[rows, :]).astype(bf16)
+        each = col_grad.shape[0] // (2 * half)
+        for i in range(2 * half):
+            attn_sum.ge[slot, i % 2, i // 2] = col_grad[i * each : (i + 1) * each, :]
+        mixed_rows = mix_t[rows, :]
+        across = width // seq_parts
+        for i in range(seq_parts):
+            block = dot_nt(mixed_rows, go_t[i * across : (i + 1) * across, :]).astype(bf16)
+            for c in range(2):
+                attn_sum.gp[slot, c, i] = block[c * each : (c + 1) * each, :]
+
+    def head_step(index, carry):
+        step = lax.div(index, group)
+        attend(place.seq_at(step + 1) * group + lax.rem(index, group))
+
+        @pl.when(index == 0)
+        def _():
+            feed_sum.core_finish(seq_parts - 1)
+            feed_sum.plane_start(seq_parts - 1)
+
+        @pl.when((lax.rem(index, group) == 0) & (index > 0))
+        def _():
+            attn_sum.core_finish(step - 1)
+            attn_sum.plane_start(step - 1)
+
+        @pl.when(lax.rem(index, group) == group - 1)
+        def _():
+            group_grads(step)
+            attn_sum.core_start(step)
+
+        @pl.when(index == COL_EVENT)
+        def _():
+            feed_sum.col_finish()
+            feed_sum.line_start(0)
+
+        @pl.when(index == ROW_EVENT)
+        def _():
+            for i in range(seq_parts):
+                feed_sum.row_finish(i)
+            feed_sum.line_start(1)
+
+        return carry
+
+    lax.fori_loop(0, HEADS, head_step, 0)
+
+    def dkv_copy(hop):
+        return remote(dkv_out.at[hop - 1], dkv_in.at[hop - 1], dk_send.at[hop - 1],
+                      dk_recv.at[hop - 1], place.plane_peer(hop))
+
+    for hop in range(1, seq_parts):
+        dkv_out[hop - 1] = dkv[hop * stretch : (hop + 1) * stretch, :].astype(bf16)
+    for hop in range(1, seq_parts):
+        dkv_copy(hop).start()
+    out_ref[...] = (base[...] + dot(mix_t[...].T, wd[...])).astype(bf16)
+    small_own[parts + 3 : parts + 4, :] = dot_nt(ones, gq_t[...])[0:1, :]
+    grad_attn = dot_nt(gq_t[...].T, wq[...])
+    attn_sum.core_finish(seq_parts - 1)
+    attn_sum.plane_start(seq_parts - 1)
+    total = dkv[0:stretch, :]
+    for hop in range(1, seq_parts):
+        dkv_copy(hop).wait()
+        total = total + dkv_in[hop - 1].astype(f32)
+    total_t = total.T
+    gkv_t = jnp.concatenate([turn(total_t[0:HD, :], -1.0), total_t[HD:, :]], axis=0).astype(bf16)
+    kv_grad = dot_nt(attn_t[...], gkv_t)
+    each = kvg.shape[2]
+    for i in range(2 * half):
+        kvg[i % 2, i // 2] = kv_grad[i * each : (i + 1) * each, :].astype(bf16)
+    kvw_sum.core_copy(kvg.at[1 - core]).start()
+    grad_attn = grad_attn + dot_nt(gkv_t.T, wkv[...])
+    small_own[parts + 4 : parts + 5, :] = jnp.sum(grad_attn * norm[...], axis=0, keepdims=True)
+    small_own[parts + 5 : parts + 6, :] = jnp.sum(grad_attn, axis=0, keepdims=True)
+    small_own[parts + 6 : parts + 7, 0 : 2 * HD] = dot_nt(ones, gkv_t)[0:1, :]
+    vec_sum.core_copy(small_own).start()
+    back = dx_ref[...] + grad_attn * again_ref[...]
+    normed = norm[...]
+    back_mean = jnp.mean(back, axis=1, keepdims=True)
+    back_dot = jnp.mean(back * normed, axis=1, keepdims=True)
+    kvw_sum.core_copy(kvg.at[1 - core]).wait()
+    kvw_sum.plane_start((kvg[core].astype(f32) + kvw_sum.cbuf[...].astype(f32)).astype(bf16))
+    vec_sum.core_copy(small_own).wait()
+    vec_sum.plane_start(small_own[...] + vec_sum.cbuf[...])
+    dx_ref[...] = go[...].astype(f32) + (back - back_mean - normed * back_dot) * rstd[:, 0:1]
+    attn_sum.col_finish()
+    attn_sum.line_start(0)
+    for i in range(seq_parts):
+        attn_sum.row_finish(i)
+    attn_sum.line_start(1)
+    eout_ref[...] = feed_sum.line_finish(0)
+    pout_ref[...] = feed_sum.line_finish(1).T
+    plane_kv = kvw_sum.plane_finish().astype(bf16)
+    for i in range(half):
+        kvz[i] = plane_kv[i]
+    kvw_sum.zbuf[line] = kvz[line]
+    for hop in range(1, half):
+        kvw_sum.line_copy(hop, kvz.at[place.line_at(hop)]).start()
+    vec_sum.zbuf[line] = vec_sum.plane_finish()
+    for hop in range(1, half):
+        vec_sum.line_copy(hop).start()
+    qout_ref[...] = attn_sum.line_finish(0)
+    dout_ref[...] = attn_sum.line_finish(1)
+    for hop in range(1, half):
+        kvw_sum.line_copy(hop, kvz.at[place.line_at(hop)]).wait()
+        vec_sum.line_copy(hop).wait()
+    summed = kvw_sum.line_sum()
+    kv_cols = kvout_ref.shape[1]
+    chosen = summed[:, 0:kv_cols]
+    for i in range(1, seq_parts):
+        chosen = jnp.where(seq == i, summed[:, i * kv_cols : (i + 1) * kv_cols], chosen)
+    kvout_ref[...] = chosen
+    small_ref[...] = vec_sum.line_sum()
+
+
+COL_EVENT = 5
+ROW_EVENT = 8
+
+
+def small_scratch(seq_parts, half, block, line_block, dtype):
+    dma = pltpu.SemaphoreType.DMA
+    return [
+        pltpu.VMEM(block, dtype), pltpu.VMEM((seq_parts,) + block, dtype),
+        pltpu.VMEM((half,) + line_block, dtype), dma((1,)), dma((1,)), dma((seq_parts - 1,)),
+        dma((seq_parts - 1,)), dma((half - 1,)), dma((half - 1,)),
+    ]
+
+
+def fast_device(
+    hidden_in, seq_lengths, attention_gain, attention_shift, feed_gain, feed_shift, query_weight,
+    query_bias, keyval_weight, keyval_bias, dense_weight, dense_bias, expand_weight, expand_bias,
+    project_weight, project_bias, out_grad,
+):
+    _, stretch, width = hidden_in.shape
+    seq_parts, dp_parts = lax.axis_size("seq"), lax.axis_size("dp")
+    half = dp_parts // 2
+    hidden_units = expand_weight.shape[1]
+    chunk = hidden_units // seq_parts
+    whole_len = stretch * seq_parts
+    positions = lax.axis_index("seq") * stretch + jnp.arange(stretch, dtype=jnp.int32)
+    half_rot = ROT // 2
+    frequency = 10000.0 ** (-2.0 * jnp.arange(half_rot, dtype=f32) / ROT)
+    angles = frequency[:, None] * positions.astype(f32)[None, :]
+    rows, cols = width // dp_parts, width // seq_parts
+    col_block, row_block = (rows, chunk), (cols, hidden_units // dp_parts)
+    vec_rows = -(-(seq_parts + 7) // 8) * 8
+    sd, dma = jax.ShapeDtypeStruct, pltpu.SemaphoreType.DMA
+
+    def vm(shape, dtype=bf16):
+        return pltpu.VMEM(shape, dtype)
+
+    in_vmem, in_hbm = pl.BlockSpec(memory_space=pltpu.VMEM), pl.BlockSpec(memory_space=pl.ANY)
+    outs = pl.pallas_call(
+        functools.partial(layer_kernel, seq_parts, half),
+        out_shape=(
+            sd((stretch, width), bf16), sd((stretch, width), f32), sd(col_block, f32),
+            sd(row_block[::-1], f32), sd((rows, cols), f32), sd((rows, cols), f32),
+            sd((rows, 2 * HD // seq_parts), f32), sd((vec_rows, width), f32),
+        ),
+        in_specs=[pl.BlockSpec(memory_space=pltpu.SMEM)] + [in_vmem] * 11 + [in_hbm] * 7,
+        out_specs=(in_vmem,) * 8,
+        scratch_shapes=[
+            vm((stretch, width)), vm((stretch, width)), vm((width, width)), vm((width, 2 * HD)),
+            vm((width, width)), vm((2, width, chunk)), vm((2, chunk, width)),
+            vm((stretch, width), f32), vm((stretch, 128), f32), vm((stretch, width)),
+            vm((width, stretch)), vm((width, stretch)), vm((width, stretch)),
+            vm((stretch, width), f32), vm((width, stretch)), vm((width, stretch)),
+            vm((width, stretch)), vm((width, stretch)), vm((seq_parts, 2 * HD, stretch)),
+            vm((HD, whole_len)), vm((HD + 16, whole_len)), vm((whole_len, 2 * HD)),
+            vm((whole_len, 2 * HD)), vm((whole_len, stretch), f32), vm((whole_len, stretch)),
+            vm((2 * HD, stretch)), vm((2 * HD, 2 * stretch)), vm((whole_len, 2 * HD), f32),
+            vm((seq_parts - 1, stretch, 2 * HD)), vm((seq_parts - 1, stretch, 2 * HD)),
+            vm((2, half, rows, 2 * HD)), vm((vec_rows, width), f32), vm((half, rows, 2 * HD)),
+            dma((9,)), dma((seq_parts - 1,)), dma((seq_parts - 1,)), dma((seq_parts - 1,)),
+            dma((seq_parts - 1,)),
+        ]
+        + reduction_scratch(seq_parts, half, col_block, row_block)
+        + reduction_scratch(seq_parts, half, (rows, cols), (rows, cols))
+        + small_scratch(seq_parts, half, (vec_rows, width), (vec_rows, width), f32)
+        + small_scratch(seq_parts, half, (half, rows, 2 * HD), (rows, 2 * HD), bf16),
+        compiler_params=pltpu.CompilerParams(
+            collective_id=0, has_side_effects=True, vmem_limit_bytes=VMEM_BYTES
+        ),
+    )(
+        seq_lengths, jnp.cos(angles), jnp.sin(angles), attention_gain[None], attention_shift[None],
+        feed_gain[None], feed_shift[None], query_bias[:, None], keyval_bias[:, None], dense_bias[None],
+        expand_bias.reshape(seq_parts, 1, chunk), project_bias[None], hidden_in[0], out_grad[0],
+        query_weight, keyval_weight, dense_weight, expand_weight, project_weight,
+    )
+    output, input_grad, expand_grad, project_grad, query_grad, dense_grad, keyval_grad, small = outs
+    n = seq_parts
+    return (
+        output[None], input_grad[None], small[n + 4], small[n + 5], small[n], small[n + 1], query_grad,
+        small[n + 3], keyval_grad, small[n + 6, : 2 * HD], dense_grad, small[n + 2], expand_grad,
+        small[:n].reshape(hidden_units), project_grad, small[n + 2],
+    )
+
+
+def fits(hidden, expand_weight):
+    seq_parts, dp_parts = lax.axis_size("seq"), lax.axis_size("dp")
+    width, hidden_units = expand_weight.shape
+    return (
+        hidden.shape[0] == 1
+        and dp_parts == 2 * seq_parts
+        and HEADS % seq_parts == 0
+        and hidden_units == seq_parts * width
+        and width % (16 * dp_parts) == 0
+        and width % (16 * seq_parts) == 0
+        and hidden_units % (128 * dp_parts) == 0
+        and hidden.shape[1] % 128 == 0
+    )
+
+
 def solution(mesh):
+    def either_way(*args):
+        return (fast_device if fits(args[0], args[12]) else per_device)(*args)
+
     return jax.shard_map(
-        per_device,
+        either_way,
         mesh=mesh,
         in_specs=(
             P("dp", "seq", None),

time: 717 us -> 144 us (0.20)
  waiting for transfers between devices: 344 us -> 0 us
  matrix products: 185 us -> 0 us
  Pallas kernels: 0 us -> 118 us
  other arithmetic: 87.4 us -> 0.77 us
  blocking collectives: 51.2 us -> 0 us
  between operations: 15.3 us -> 1.35 us
    reduce_scatter x7 -> x0, waiting for transfers between devices: 292 us -> none  [the longest x1 98.2 us: per_device(): lax.psum_scatter(expand_term, 'dp', scatter_dimension=0, tiled=True)]
    dot_general x33 -> x0, matrix products: 185 us -> none  [the longest x3 38.3 us: one_group(): jnp.einsum('gtd,sd->gts', grad_grp, values, preferred_element_type=jnp.fl...]
    pallas_call x0 -> x1, Pallas kernels: none -> 118 us  [fast_device(): pl.pallas_call(functools.partial(layer_kernel, seq_parts, half), out_shap...]
    unnamed x15 -> x0, waiting for transfers between devices: 51.7 us -> none
    convert_element_type x4 -> x1, other arithmetic: 49.5 us -> 0.01 us  [fast_device(): angles = frequency[:, None] * positions.astype(f32)[None, :]]
    psum x1 -> x0, blocking collectives: 39.7 us -> none  [per_device(): lax.psum((attn_dgain, attn_dshift, feed_dgain, feed_dshift, jnp.sum(grad_...]
    reduce_sum x10 -> x0, other arithmetic: 25.4 us -> none  [the longest x3 12.1 us: one_group(): log_total = jax.nn.logsumexp(scores, axis=-1, keepdims=True)]
    all_gather x1 -> x0, blocking collectives: 11.5 us -> none  [per_device(): gathered = lax.all_gather(keyval_low, 'seq', axis=1, tiled=True)]
  transfers between devices with their start and end apart: 11 -> 0, of which waited for: 8 -> 0; matrix products, arithmetic and copies ran while one was open for 13% -> 0% of each run, Pallas kernels for 0% -> 0%
where the time goes in v2:
time: 144 us
  Pallas kernels  118 us (82%)
  local copies, waits for them, and re-layouts  23.9 us (17%)
    pallas_call x1, Pallas kernels, fast_device(): pl.pallas_call(functools.partial(layer_kernel, seq_parts, half), out_shap...  118 us
    unnamed x18, local copies, waits for them, and re-layouts  9.15 us

profile of v2, /device:TPU:0, one launch (start us, length us, event | category | flops | bytes accessed | tf_op | source)
XLA Modules:
  0.0 143.7 jit_solution(8822435587163501851)
XLA Ops:
  0.7 0.8 multiply_sine_fusion
  1.4 1.6 %broadcast_in_dim.42.refs_7_ = f32[768,1]{1,0:T(8,128)} reshape(f32[768]{0:T(1024)} %param.24) | data formatting | bytes 6144 | tf_op jit(solution)/shard_map/broadcast_in_dim | solution.py:835
  3.0 1.4 copy.37.refs_8_
  4.4 1.3 broadcast_in_dim.32.refs_3_
  5.7 1.3 broadcast_in_dim.33.refs_4_
  7.0 1.3 broadcast_in_dim.34.refs_5_
  8.2 1.3 broadcast_in_dim.35.refs_6_
  9.5 1.3 broadcast_in_dim.38.refs_9_
  10.8 1.3 broadcast_in_dim.39.refs_11_
  12.7 117.7 %shard_map.288 = (bf16[512,768]{1,0:T(8,128)(2,1)}, f32[512,768]{1,0:T(8,128)}, f32[96,768]{1,0:T(8,128)}, f32[384,192]{1,0:T(8,128)}, f32[96,192]{1,0:T(8,128)}...) custom-call(s32[1]{0:T(128)S(6)} %copy.46.refs_0_, f32[8,512]{1,0:T(8,128)} %get-tuple-element.71.refs_1_, ...), custom_call_target="tpu_custom_call" | custom-call | tf_op jit(solution)/shard_map/pallas_call | solution.py:802
  130.3 0.0 copy-start
  130.4 1.6 %slice_reduce_fusion = (f32[768]{0:T(1024)S(1)}, f32[768]{0:T(1024)}, f32[768]{0:T(1024)}, f32[768]{0:T(1024)}, f32[768]{0:T(1024)}, /*index=5*/f32[768]{0:T(1024)}) fusion(f32[16,768]{1,0:T(8,128)} %get-tuple-element.26), kind=kLoop, calls=%fused_computation.2 | loop fusion | bytes 36864 | tf_op jit(solution)/shard_map/slice | solution.py:843
  132.0 0.0 copy-start.4
  132.0 0.7 slice.32
  132.7 0.6 reshape.49
  133.3 1.2 slice_bitcast_fusion
  134.5 1.9 %copy.39 = f32[384,192]{0,1:T(8,128)} copy(f32[384,192]{1,0:T(8,128)} %get-tuple-element.62) | data formatting | bytes 589824
  136.4 1.5 %copy.38 = f32[96,32]{0,1:T(8,128)} copy(f32[96,32]{1,0:T(8,128)} %get-tuple-element.56) | data formatting | bytes 24576
  137.8 0.6 copy.47
  138.4 2.1 %copy.48 = bf16[1,512,768]{2,1,0:T(8,128)(2,1)} copy(bf16[1,512,768]{2,1,0:T(8,128)(2,1)} %bitcast.9) | data formatting | bytes 1572864
  140.5 0.0 copy-done
  140.5 0.0 copy-start.3
  140.5 0.0 copy-start.2
  140.5 0.0 copy-start.1
  140.5 1.1 copy.49
  141.7 0.0 copy-done.4
  141.7 0.0 copy-done.3
  141.7 0.6 copy.50
  142.3 0.0 copy-done.2
  142.3 0.6 copy.51
  143.0 0.0 copy-done.1
  143.0 0.7 copy.52
  (2 shorter events, 0.0 us)
Async XLA Ops:
  130.3 10.2 %copy-start = (f32[512,768]{1,0:T(8,128)S(1)}, f32[512,768]{1,0:T(8,128)}, u32[]{:S(2)}) copy-start(f32[512,768]{1,0:T(8,128)} %get-tuple-element.25) | copy-start | bytes 4718596
  132.0 9.7 %copy-start.4 = (f32[768]{0:T(1024)}, f32[768]{0:T(1024)S(1)}, u32[]{:S(2)}) copy-start(f32[768]{0:T(1024)S(1)} %get-tuple-element.131) | copy-start | bytes 9220
  140.5 1.2 copy-start.3
  140.5 1.8 %copy-start.2 = (f32[96,192]{1,0:T(8,128)S(1)}, f32[96,192]{1,0:T(8,128)}, u32[]{:S(2)}) copy-start(f32[96,192]{1,0:T(8,128)} %get-tuple-element.130) | copy-start | bytes 221188
  140.5 2.4 %copy-start.1 = (f32[96,768]{1,0:T(8,128)S(1)}, f32[96,768]{1,0:T(8,128)}, u32[]{:S(2)}) copy-start(f32[96,768]{1,0:T(8,128)} %get-tuple-element.132) | copy-start | bytes 884740

commit v3 on v2

--- a/solution.py
+++ b/solution.py
@@ -274,6 +274,14 @@
     def line_at(self, hop):
         return lax.rem(self.line + hop, self.half)
 
+    def flip(self, mask):
+        return {"seq": self.swapped(mask)}
+
+    def swapped(self, mask):
+        low, high = lax.rem(self.seq, 2), lax.div(self.seq, 2)
+        low = lax.rem(low + lax.rem(mask, 2), 2)
+        return low + 2 * lax.rem(high + lax.div(mask, 2), 2)
+
     def plane_peer(self, hop):
         return {"seq": self.seq_at(hop)}
 
@@ -291,8 +299,7 @@
 class Reduction:
     def __init__(self, place, bufs, sems):
         self.at = place
-        (self.ge, self.gp, self.ce, self.cp, self.pe, self.pp, self.te, self.tp, self.le,
-         self.lp) = bufs
+        self.ge, self.gp, self.ce, self.cp, self.pe, self.pp, self.sums, self.landed = bufs
         (self.cs, self.cr, self.es, self.er, self.ps, self.pr, self.zs, self.zr) = sems
 
     def core_copies(self, step):
@@ -334,40 +341,40 @@
         for hop in range(1, self.at.seq_parts):
             self.row_copy(step, hop).start()
 
-    def col_finish(self):
-        last = self.at.seq_parts - 1
+    def sum_finish(self):
+        at, last = self.at, self.at.seq_parts - 1
         for step in range(last):
             self.col_copy(step).wait()
-        for i in range(self.at.half):
+        for step in range(at.seq_parts):
+            for hop in range(1, at.seq_parts):
+                self.row_copy(step, hop).wait()
+        split = self.ce.shape[-1]
+        for i in range(at.half):
             total = self.ce[last, i].astype(f32)
             for step in range(last):
                 total = total + self.pe[step, i].astype(f32)
-            self.te[i] = total.astype(bf16)
-
-    def row_finish(self, step):
-        at, part = self.at, self.at.seq_at(step + 1)
-        total = self.cp[step, at.seq].astype(f32)
-        for hop in range(1, at.seq_parts):
-            self.row_copy(step, hop).wait()
-            total = total + self.pp[part, hop - 1].astype(f32)
-        self.tp[part] = total.astype(bf16)
-
-    def line_copy(self, family, hop):
+            self.sums[i, :, 0:split] = total.astype(bf16)
+        for step in range(at.seq_parts):
+            part = at.seq_at(step + 1)
+            total = self.cp[step, at.seq].astype(f32)
+            for hop in range(1, at.seq_parts):
+                total = total + self.pp[part, hop - 1].astype(f32)
+            self.sums[part, :, split:] = total.astype(bf16)
+
+    def line_copy(self, hop):
         at = self.at
-        src, dst = ((self.te, self.le), (self.tp, self.lp))[family]
-        return remote(src.at[at.line_at(hop)], dst.at[hop - 1], self.zs.at[family, hop - 1],
-                      self.zr.at[family, hop - 1], at.line_peer(hop))
-
-    def line_start(self, family):
+        return remote(self.sums.at[at.line_at(hop)], self.landed.at[hop - 1], self.zs.at[hop - 1],
+                      self.zr.at[hop - 1], at.line_peer(hop))
+
+    def line_start(self):
         for hop in range(1, self.at.half):
-            self.line_copy(family, hop).start()
-
-    def line_finish(self, family):
-        src, dst = ((self.te, self.le), (self.tp, self.lp))[family]
-        total = src[self.at.line].astype(f32)
+            self.line_copy(hop).start()
+
+    def line_finish(self):
+        total = self.sums[self.at.line].astype(f32)
         for hop in range(1, self.at.half):
-            self.line_copy(family, hop).wait()
-            total = total + dst[hop - 1].astype(f32)
+            self.line_copy(hop).wait()
+            total = total + self.landed[hop - 1].astype(f32)
         return total
 
 
@@ -378,31 +385,113 @@
         (2, 2, half) + col_block, (2, 2, seq_parts) + row_block,
         (seq_parts, half) + col_block, (seq_parts, seq_parts) + row_block,
         (hops, half) + col_block, (seq_parts, hops) + row_block,
-        (half,) + col_block, (half,) + row_block,
-        (legs,) + col_block, (legs,) + row_block,
+        (half, col_block[0], col_block[1] + row_block[1]),
+        (legs, col_block[0], col_block[1] + row_block[1]),
     ]
     sems = [
         dma((seq_parts, 2)), dma((seq_parts, 2)), dma((hops,)), dma((hops,)),
-        dma((seq_parts, hops)), dma((seq_parts, hops)), dma((2, legs)), dma((2, legs)),
+        dma((seq_parts, hops)), dma((seq_parts, hops)), dma((legs,)), dma((legs,)),
     ]
     return [pltpu.VMEM(shape, bf16) for shape in bufs] + sems
 
 
+class TreeSum:
+    def __init__(self, place, bufs, sems):
+        self.at = place
+        self.made, self.core, self.via, self.side, self.sums, self.landed = bufs
+        self.cs, self.cr, self.vs, self.vr, self.ss, self.sr, self.zs, self.zr = sems
+        self.half = self.at.half // 2
+
+    def core_copy(self, step):
+        at, slot = self.at, lax.rem(step, 2)
+        return remote(self.made.at[slot, 1 - at.core], self.core.at[step], self.cs.at[step],
+                      self.cr.at[step], at.partner)
+
+    def core_finish(self, step):
+        at, slot = self.at, lax.rem(step, 2)
+        self.core_copy(step).wait()
+        for i in range(at.half):
+            self.core[step, i] = (
+                self.made[slot, at.core, i].astype(f32) + self.core[step, i].astype(f32)
+            ).astype(bf16)
+
+    def via_copy(self, side):
+        span = pl.ds(side * self.half, self.half)
+        return remote(self.core.at[0, span], self.via.at[side], self.vs.at[side], self.vr.at[side],
+                      self.at.flip(1 + side))
+
+    def via_start(self):
+        for side in range(2):
+            self.via_copy(side).start()
+
+    def side_copy(self, side):
+        return remote(self.core.at[1 + side], self.side.at[side], self.ss.at[side],
+                      self.sr.at[side], self.at.flip(2 - side))
+
+    def side_start(self):
+        for side in range(2):
+            self.via_copy(side).wait()
+            for i in range(self.half):
+                j = side * self.half + i
+                self.core[1 + side, j] = (
+                    self.core[1 + side, j].astype(f32) + self.via[side, i].astype(f32)
+                ).astype(bf16)
+        for side in range(2):
+            self.side_copy(side).start()
+
+    def side_finish(self):
+        for side in range(2):
+            self.side_copy(side).wait()
+        for i in range(self.at.half):
+            self.sums[i] = (
+                self.core[3, i].astype(f32) + self.side[0, i].astype(f32) + self.side[1, i].astype(f32)
+            ).astype(bf16)
+
+    def line_copy(self, hop):
+        at = self.at
+        return remote(self.sums.at[at.line_at(hop)], self.landed.at[hop - 1], self.zs.at[hop - 1],
+                      self.zr.at[hop - 1], at.line_peer(hop))
+
+    def line_start(self):
+        for hop in range(1, self.at.half):
+            self.line_copy(hop).start()
+
+    def line_finish(self):
+        total = self.sums[self.at.line].astype(f32)
+        for hop in range(1, self.at.half):
+            self.line_copy(hop).wait()
+            total = total + self.landed[hop - 1].astype(f32)
+        return total
+
+
+def tree_scratch(half, block):
+    dma = pltpu.SemaphoreType.DMA
+    bufs = [
+        (2, 2, half) + block, (4, half) + block, (2, half // 2) + block, (2, half) + block,
+        (half,) + block, (half - 1,) + block,
+    ]
+    return [pltpu.VMEM(shape, bf16) for shape in bufs] + [
+        dma((4,)), dma((4,)), dma((2,)), dma((2,)), dma((2,)), dma((2,)), dma((half - 1,)),
+        dma((half - 1,)),
+    ]
+
+
 class Small:
-    def __init__(self, place, cbuf, pbuf, zbuf, sems):
-        self.at, self.cbuf, self.pbuf, self.zbuf = place, cbuf, pbuf, zbuf
+    def __init__(self, place, own, cbuf, pbuf, zbuf, sems):
+        self.at, self.own, self.cbuf, self.pbuf, self.zbuf = place, own, cbuf, pbuf, zbuf
         self.cs, self.cr, self.ps, self.pr, self.zs, self.zr = sems
 
-    def core_copy(self, src):
-        return remote(src, self.cbuf, self.cs.at[0], self.cr.at[0], self.at.partner)
+    def core_copy(self):
+        return remote(self.own, self.cbuf, self.cs.at[0], self.cr.at[0], self.at.partner)
 
     def plane_copy(self, hop):
         at = self.at
         mine = self.pbuf.at[at.seq]
         return remote(mine, mine, self.ps.at[hop - 1], self.pr.at[hop - 1], at.plane_peer(hop))
 
-    def plane_start(self, value):
-        self.pbuf[self.at.seq] = value
+    def plane_start(self):
+        self.core_copy().wait()
+        self.pbuf[self.at.seq] = self.own[...] + self.cbuf[...]
         for hop in range(1, self.at.seq_parts):
             self.plane_copy(hop).start()
 
@@ -414,19 +503,85 @@
             total = total + self.pbuf[i].astype(f32)
         return total
 
-    def line_copy(self, hop, src=None):
+    def line_copy(self, hop):
         at = self.at
         mine = self.zbuf.at[at.line]
-        return remote(mine if src is None else src, mine, self.zs.at[hop - 1], self.zr.at[hop - 1],
-                      at.line_peer(hop))
+        return remote(mine, mine, self.zs.at[hop - 1], self.zr.at[hop - 1], at.line_peer(hop))
+
+    def line_start(self):
+        self.zbuf[self.at.line] = self.plane_finish()
+        for hop in range(1, self.at.half):
+            self.line_copy(hop).start()
 
     def line_sum(self):
+        for hop in range(1, self.at.half):
+            self.line_copy(hop).wait()
         total = self.zbuf[0].astype(f32)
         for i in range(1, self.at.half):
             total = total + self.zbuf[i].astype(f32)
         return total
 
 
+class KeyvalSum:
+    def __init__(self, place, bufs, sems):
+        self.at = place
+        self.made, self.core, self.side, self.sums, self.landed = bufs
+        self.cs, self.cr, self.ps, self.pr, self.zs, self.zr = sems
+
+    def core_copy(self):
+        return remote(self.made.at[1 - self.at.core], self.core, self.cs.at[0], self.cr.at[0],
+                      self.at.partner)
+
+    def plane_copy(self, hop):
+        return remote(self.core.at[self.at.seq_at(hop)], self.side.at[hop - 1], self.ps.at[hop - 1],
+                      self.pr.at[hop - 1], self.at.plane_peer(hop))
+
+    def core_finish(self):
+        self.core_copy().wait()
+        self.core[...] = (
+            self.made[self.at.core].astype(f32) + self.core[...].astype(f32)
+        ).astype(bf16)
+
+    def plane_start(self):
+        for hop in range(1, self.at.seq_parts):
+            self.plane_copy(hop).start()
+
+    def plane_finish(self):
+        total = self.core[self.at.seq].astype(f32)
+        for hop in range(1, self.at.seq_parts):
+            self.plane_copy(hop).wait()
+            total = total + self.side[hop - 1].astype(f32)
+        self.sums[...] = total.astype(bf16)
+
+    def line_copy(self, hop):
+        at = self.at
+        return remote(self.sums.at[at.line_at(hop)], self.landed.at[hop - 1], self.zs.at[hop - 1],
+                      self.zr.at[hop - 1], at.line_peer(hop))
+
+    def line_start(self):
+        for hop in range(1, self.at.half):
+            self.line_copy(hop).start()
+
+    def line_finish(self):
+        total = self.sums[self.at.line].astype(f32)
+        for hop in range(1, self.at.half):
+            self.line_copy(hop).wait()
+            total = total + self.landed[hop - 1].astype(f32)
+        return total
+
+
+def keyval_scratch(seq_parts, half, block):
+    dma = pltpu.SemaphoreType.DMA
+    bufs = [
+        (2, seq_parts, half) + block, (seq_parts, half) + block, (seq_parts - 1, half) + block,
+        (half,) + block, (half - 1,) + block,
+    ]
+    return [pltpu.VMEM(shape, bf16) for shape in bufs] + [
+        dma((1,)), dma((1,)), dma((seq_parts - 1,)), dma((seq_parts - 1,)), dma((half - 1,)),
+        dma((half - 1,)),
+    ]
+
+
 def layer_kernel(seq_parts, half, *refs):
     refs = list(refs)
 
@@ -434,25 +589,26 @@
         taken, refs[:count] = refs[:count], []
         return taken
 
-    (length_ref, cos_ref, sin_ref, again_ref, ashift_ref, fgain_ref, fshift_ref, qbias_ref,
-     kvbias_ref, dbias_ref, ebias_ref, pbias_ref) = take(12)
+    (length_ref, again_ref, ashift_ref, fgain_ref, fshift_ref, qbias_ref, kvbias_ref, dbias_ref,
+     ebias_ref, pbias_ref) = take(10)
     hid_hbm, og_hbm, wq_hbm, wkv_hbm, wd_hbm, we_hbm, wp_hbm = take(7)
-    out_ref, dx_ref, eout_ref, pout_ref, qout_ref, dout_ref, kvout_ref, small_ref = take(8)
+    out_hbm, dx_hbm, eout_hbm, pout_hbm, qd_ref, kvout_ref, feed_small_ref, attn_small_ref = take(8)
     (hid, go, wq, wkv, wd, we, wp, norm, rstd, feed, feed_t, go_t, attn_t, base, query_t, gm_t, mix_t,
-     gq_t, kvt, kt, vt, kaug, kv, score, expo, qaug, pair, dkv, dkv_out, dkv_in, kvg, small_own,
-     kvz) = take(33)
-    load_sem, kv_send, kv_recv, dk_send, dk_recv = take(5)
+     gq_t, active_all, kvt, kt, vt, kaug, kv, score, expo, qaug, pair, dkv, dkv_out, dkv_in, ebias,
+     turns, dx, eout, pout) = take(36)
+    load_sem, store_sem, kv_send, kv_recv, dk_send, dk_recv = take(6)
     place = Place(seq_parts, half)
-    feed_sum = Reduction(place, take(10), take(8))
-    attn_sum = Reduction(place, take(10), take(8))
-    vec_sum = Small(place, *take(3), take(6))
-    kvw_sum = Small(place, *take(3), take(6))
-    seq, core, line = place.seq, place.core, place.line
+    expand_sum = TreeSum(place, take(6), take(8))
+    project_sum = TreeSum(place, take(6), take(8))
+    attn_sum = Reduction(place, take(8), take(8))
+    feed_small = Small(place, *take(4), take(6))
+    attn_small = Small(place, *take(4), take(6))
+    keyval_sum = KeyvalSum(place, take(5), take(6))
+    seq = place.seq
     stretch, width = hid.shape
     chunk = we.shape[2]
-    col_rows = feed_sum.ge.shape[3]
-    row_rows = feed_sum.gp.shape[3]
-    row_cols = feed_sum.gp.shape[4]
+    col_rows = expand_sum.made.shape[3]
+    row_rows, row_cols = project_sum.made.shape[3:]
     group = HEADS // seq_parts
     group_rows = group * HD
     half_rot = ROT // 2
@@ -463,13 +619,13 @@
 
     def load_chunk(step):
         slot = lax.rem(step, 2)
-        start = place.seq_at(step + 1) * chunk
+        start = place.swapped(3 - step) * chunk
         return (
             load(we_hbm.at[:, aligned(start, chunk, 128)], we.at[slot], 5 + 2 * slot),
             load(wp_hbm.at[aligned(start, chunk, 16), :], wp.at[slot], 6 + 2 * slot),
         )
 
-    loads = (load(hid_hbm, hid, 0), load(wkv_hbm, wkv, 1), load(wq_hbm, wq, 2), load(og_hbm, go, 3),
+    loads = (load(hid_hbm.at[0], hid, 0), load(wkv_hbm, wkv, 1), load(wq_hbm, wq, 2), load(og_hbm.at[0], go, 3),
              load(wd_hbm, wd, 4))
     for copy in loads:
         copy.start()
@@ -482,6 +638,15 @@
         pl.semaphore_signal(barrier, inc=1, device_id=place.plane_peer(hop), device_id_type=MESH_ID)
     for hop in range(1, half):
         pl.semaphore_signal(barrier, inc=1, device_id=place.line_peer(hop), device_id_type=MESH_ID)
+
+    def row(ref):
+        return ref[...].reshape(1, ref.shape[0])
+
+    def column(ref):
+        return jnp.broadcast_to(row(ref), (128, ref.shape[0])).T[:, 0:1]
+
+    def store(src, dst, index):
+        return pltpu.make_async_copy(src, dst, store_sem.at[index])
 
     length = length_ref[0]
     loads[0].wait()
@@ -492,22 +657,33 @@
     normed = centered * inverse
     norm[...] = normed
     rstd[...] = jnp.broadcast_to(inverse, rstd.shape)
-    base[...] = values + (dbias_ref[...] + pbias_ref[...])
-    attn_t[...] = (normed * again_ref[...] + ashift_ref[...]).astype(bf16).T
-    low = (normed * fgain_ref[...] + fshift_ref[...]).astype(bf16)
+    base[...] = values + (row(dbias_ref) + row(pbias_ref))
+    attn_t[...] = (normed * row(again_ref) + row(ashift_ref)).astype(bf16).T
+    low = (normed * row(fgain_ref) + row(fshift_ref)).astype(bf16)
     feed[...] = low
     feed_t[...] = low.T
 
+    for i in range(seq_parts):
+        ebias[i : i + 1, :] = ebias_ref[i * chunk : (i + 1) * chunk].reshape(1, chunk)
+    which = lax.broadcasted_iota(jnp.int32, (half_rot, stretch), 0)
+    spot = (seq * stretch + lax.broadcasted_iota(jnp.int32, (half_rot, stretch), 1)).astype(f32)
+    frequency = jnp.zeros((half_rot, stretch), f32)
+    for i in range(half_rot):
+        frequency = jnp.where(which == i, 10000.0 ** (-2.0 * i / ROT), frequency)
+    whole_cos, whole_sin = jnp.cos(spot * frequency), jnp.sin(spot * frequency)
+    turns[0:half_rot, :] = whole_cos
+    turns[half_rot:, :] = whole_sin
+
     def turn(rows, direction):
         lead, pair_part = rows[0:half_rot, :], rows[half_rot:ROT, :]
-        cosine, sine = cos_ref[...], sin_ref[...] * direction
+        cosine, sine = turns[0:half_rot, :], turns[half_rot:, :] * direction
         return jnp.concatenate(
             [lead * cosine - pair_part * sine, pair_part * cosine + lead * sine, rows[ROT:, :]], axis=0
         )
 
     loads[1].wait()
     own = lax.dot_general(wkv[...], attn_t[...], (((0,), (0,)), ((), ())),
-                          preferred_element_type=f32) + kvbias_ref[...]
+                          preferred_element_type=f32) + column(kvbias_ref)
     kvt[0] = jnp.concatenate([turn(own[0:HD, :], 1.0), own[HD:, :]], axis=0).astype(bf16)
 
     def kv_copy(hop):
@@ -517,11 +693,12 @@
     pl.semaphore_wait(barrier, seq_parts + half - 1)
     loads[2].wait()
     wq_t = wq[...].T
+    query_bias = column(qbias_ref)
     for hop in range(1, seq_parts):
         kv_copy(hop).start()
     for head in range(HEADS):
         span = slice(head * HD, (head + 1) * HD)
-        rows = dot(wq_t[span, :], attn_t[...]) + qbias_ref[span, :]
+        rows = dot(wq_t[span, :], attn_t[...]) + query_bias[span, :]
         query_t[span, :] = (turn(rows, 1.0) * scale).astype(bf16)
 
     loads[3].wait()
@@ -532,15 +709,17 @@
     loads[4].wait()
     gm_t[...] = dot(wd[...], go_t[...]).astype(bf16)
     ones = jnp.ones((16, stretch), bf16)
-    small_own[...] = jnp.zeros(small_own.shape, f32)
+    feed_own, attn_own = feed_small.own, attn_small.own
+    feed_own[...] = jnp.zeros(feed_own.shape, f32)
+    attn_own[...] = jnp.zeros(attn_own.shape, f32)
     parts = seq_parts
-    small_own[parts + 2 : parts + 3, :] = dot(ones, go[...])[0:1, :]
-
-    dx_ref[...] = jnp.zeros(dx_ref.shape, f32)
+    feed_own[parts + 2 : parts + 3, :] = dot(ones, go[...])[0:1, :]
+
+    dx[...] = jnp.zeros(dx.shape, f32)
 
     def feed_step(step, carry):
         slot = lax.rem(step, 2)
-        part = place.seq_at(step + 1)
+        part = place.swapped(3 - step)
 
         @pl.when(step + 1 < seq_parts)
         def _():
@@ -549,42 +728,66 @@
 
         for copy in load_chunk(step):
             copy.wait()
-        upper = dot(feed[...], we[slot]) + ebias_ref[part]
+        upper = dot(feed[...], we[slot]) + ebias[pl.ds(part, 1), :]
         grad_active = dot_nt(go[...], wp[slot])
         share = 0.5 * (1.0 + lax.erf(upper * (0.5**0.5)))
         slope = share + upper * (jnp.exp(-0.5 * upper * upper) * 0.3989422804014327)
         active = (upper * share).astype(bf16)
+        active_all[:, aligned(part * chunk, chunk, 128)] = active
         grad_upper = (grad_active * slope).astype(bf16)
         col_grad = dot(feed_t[...], grad_upper).astype(bf16)
         for i in range(2 * half):
-            feed_sum.ge[slot, i % 2, i // 2] = col_grad[i * col_rows : (i + 1) * col_rows, :]
-        row_grad = dot(go_t[...], active).astype(bf16)
-        for c in range(2):
-            for i in range(seq_parts):
-                feed_sum.gp[slot, c, i] = row_grad[
-                    i * row_rows : (i + 1) * row_rows, c * row_cols : (c + 1) * row_cols
-                ]
-        small_own[pl.ds(part, 1), :] = dot(ones, grad_upper)[0:1, :]
+            expand_sum.made[slot, i % 2, i // 2] = col_grad[i * col_rows : (i + 1) * col_rows, :]
+        feed_own[pl.ds(part, 1), :] = dot(ones, grad_upper)[0:1, :]
 
         @pl.when(step > 0)
         def _():
-            feed_sum.core_finish(step - 1)
+            expand_sum.core_finish(step - 1)
 
         base[...] += dot(active, wp[slot])
-        dx_ref[...] += dot_nt(grad_upper, we[slot])
-
-        @pl.when(step > 0)
-        def _():
-            feed_sum.plane_start(step - 1)
-
-        feed_sum.core_start(step)
+        dx[...] += dot_nt(grad_upper, we[slot])
+
+        @pl.when(step == 1)
+        def _():
+            expand_sum.via_start()
+
+        @pl.when(step == 3)
+        def _():
+            expand_sum.side_start()
+
+        expand_sum.core_copy(step).start()
         return carry
 
     lax.fori_loop(0, seq_parts, feed_step, 0)
-    grad_feed = dx_ref[...]
-    small_own[parts : parts + 1, :] = jnp.sum(grad_feed * norm[...], axis=0, keepdims=True)
-    small_own[parts + 1 : parts + 2, :] = jnp.sum(grad_feed, axis=0, keepdims=True)
-    dx_ref[...] = grad_feed * fgain_ref[...]
+
+    def project_step(step, carry):
+        slot = lax.rem(step, 2)
+
+        @pl.when(step == 1)
+        def _():
+            expand_sum.core_finish(3)
+
+        @pl.when(step > 1)
+        def _():
+            project_sum.core_finish(step - 2)
+
+        rows = aligned(place.swapped(3 - step) * row_rows, row_rows, 16)
+        row_grad = dot(go_t[rows, :], active_all[...]).astype(bf16)
+        for i in range(2 * half):
+            project_sum.made[slot, i % 2, i // 2] = row_grad[:, i * row_cols : (i + 1) * row_cols]
+
+        @pl.when(step == 2)
+        def _():
+            project_sum.via_start()
+
+        project_sum.core_copy(step).start()
+        return carry
+
+    lax.fori_loop(0, seq_parts, project_step, 0)
+    grad_feed = dx[...]
+    feed_own[parts : parts + 1, :] = jnp.sum(grad_feed * norm[...], axis=0, keepdims=True)
+    feed_own[parts + 1 : parts + 2, :] = jnp.sum(grad_feed, axis=0, keepdims=True)
+    dx[...] = grad_feed * row(fgain_ref)
 
     lane = lax.broadcasted_iota(jnp.int32, (16, stretch), 1)
     first = lax.broadcasted_iota(jnp.int32, (16, stretch), 0) == 0
@@ -666,29 +869,41 @@
 
         @pl.when(index == 0)
         def _():
-            feed_sum.core_finish(seq_parts - 1)
-            feed_sum.plane_start(seq_parts - 1)
+            project_sum.core_finish(2)
+            project_sum.core_finish(3)
+            expand_sum.side_finish()
+            expand_sum.line_start()
+
+        @pl.when(index == 2)
+        def _():
+            feed_small.core_copy().start()
+
+        @pl.when(index == 3)
+        def _():
+            feed_small.plane_start()
+
+        @pl.when(index == 4)
+        def _():
+            feed_small.line_start()
+
+        @pl.when(index == SIDE_EVENT)
+        def _():
+            project_sum.side_start()
+
+        @pl.when(index == LINE_EVENT)
+        def _():
+            project_sum.side_finish()
+            project_sum.line_start()
 
         @pl.when((lax.rem(index, group) == 0) & (index > 0))
         def _():
             attn_sum.core_finish(step - 1)
             attn_sum.plane_start(step - 1)
 
-        @pl.when(lax.rem(index, group) == group - 1)
+        @pl.when((lax.rem(index, group) == group - 1) & (index < HEADS - 1))
         def _():
             group_grads(step)
             attn_sum.core_start(step)
-
-        @pl.when(index == COL_EVENT)
-        def _():
-            feed_sum.col_finish()
-            feed_sum.line_start(0)
-
-        @pl.when(index == ROW_EVENT)
-        def _():
-            for i in range(seq_parts):
-                feed_sum.row_finish(i)
-            feed_sum.line_start(1)
 
         return carry
 
@@ -702,75 +917,104 @@
         dkv_out[hop - 1] = dkv[hop * stretch : (hop + 1) * stretch, :].astype(bf16)
     for hop in range(1, seq_parts):
         dkv_copy(hop).start()
-    out_ref[...] = (base[...] + dot(mix_t[...].T, wd[...])).astype(bf16)
-    small_own[parts + 3 : parts + 4, :] = dot_nt(ones, gq_t[...])[0:1, :]
+    last = seq_parts - 1
+    group_grads(last)
+    attn_sum.core_start(last)
+    feed[...] = (base[...] + dot(mix_t[...].T, wd[...])).astype(bf16)
+    attn_own[2:3, :] = dot_nt(ones, gq_t[...])[0:1, :]
     grad_attn = dot_nt(gq_t[...].T, wq[...])
-    attn_sum.core_finish(seq_parts - 1)
-    attn_sum.plane_start(seq_parts - 1)
+    attn_sum.core_finish(last)
+    attn_sum.plane_start(last)
+    stores = [store(feed, out_hbm.at[0], 0)]
+    stores[0].start()
     total = dkv[0:stretch, :]
     for hop in range(1, seq_parts):
         dkv_copy(hop).wait()
         total = total + dkv_in[hop - 1].astype(f32)
     total_t = total.T
     gkv_t = jnp.concatenate([turn(total_t[0:HD, :], -1.0), total_t[HD:, :]], axis=0).astype(bf16)
-    kv_grad = dot_nt(attn_t[...], gkv_t)
-    each = kvg.shape[2]
+    kv_each, each = keyval_sum.made.shape[3:]
     for i in range(2 * half):
-        kvg[i % 2, i // 2] = kv_grad[i * each : (i + 1) * each, :].astype(bf16)
-    kvw_sum.core_copy(kvg.at[1 - core]).start()
+        block = dot_nt(gkv_t, attn_t[i * each : (i + 1) * each, :]).astype(bf16)
+        for j in range(seq_parts):
+            keyval_sum.made[i % 2, j, i // 2] = block[j * kv_each : (j + 1) * kv_each, :]
+    keyval_sum.core_copy().start()
     grad_attn = grad_attn + dot_nt(gkv_t.T, wkv[...])
-    small_own[parts + 4 : parts + 5, :] = jnp.sum(grad_attn * norm[...], axis=0, keepdims=True)
-    small_own[parts + 5 : parts + 6, :] = jnp.sum(grad_attn, axis=0, keepdims=True)
-    small_own[parts + 6 : parts + 7, 0 : 2 * HD] = dot_nt(ones, gkv_t)[0:1, :]
-    vec_sum.core_copy(small_own).start()
-    back = dx_ref[...] + grad_attn * again_ref[...]
+    attn_own[0:1, :] = jnp.sum(grad_attn * norm[...], axis=0, keepdims=True)
+    attn_own[1:2, :] = jnp.sum(grad_attn, axis=0, keepdims=True)
+    attn_own[3:4, 0 : 2 * HD] = dot_nt(ones, gkv_t)[0:1, :]
+    attn_small.core_copy().start()
+    attn_sum.sum_finish()
+    attn_sum.line_start()
+    back = dx[...] + grad_attn * row(again_ref)
     normed = norm[...]
     back_mean = jnp.mean(back, axis=1, keepdims=True)
     back_dot = jnp.mean(back * normed, axis=1, keepdims=True)
-    kvw_sum.core_copy(kvg.at[1 - core]).wait()
-    kvw_sum.plane_start((kvg[core].astype(f32) + kvw_sum.cbuf[...].astype(f32)).astype(bf16))
-    vec_sum.core_copy(small_own).wait()
-    vec_sum.plane_start(small_own[...] + vec_sum.cbuf[...])
-    dx_ref[...] = go[...].astype(f32) + (back - back_mean - normed * back_dot) * rstd[:, 0:1]
-    attn_sum.col_finish()
-    attn_sum.line_start(0)
-    for i in range(seq_parts):
-        attn_sum.row_finish(i)
-    attn_sum.line_start(1)
-    eout_ref[...] = feed_sum.line_finish(0)
-    pout_ref[...] = feed_sum.line_finish(1).T
-    plane_kv = kvw_sum.plane_finish().astype(bf16)
-    for i in range(half):
-        kvz[i] = plane_kv[i]
-    kvw_sum.zbuf[line] = kvz[line]
-    for hop in range(1, half):
-        kvw_sum.line_copy(hop, kvz.at[place.line_at(hop)]).start()
-    vec_sum.zbuf[line] = vec_sum.plane_finish()
-    for hop in range(1, half):
-        vec_sum.line_copy(hop).start()
-    qout_ref[...] = attn_sum.line_finish(0)
-    dout_ref[...] = attn_sum.line_finish(1)
-    for hop in range(1, half):
-        kvw_sum.line_copy(hop, kvz.at[place.line_at(hop)]).wait()
-        vec_sum.line_copy(hop).wait()
-    summed = kvw_sum.line_sum()
-    kv_cols = kvout_ref.shape[1]
-    chosen = summed[:, 0:kv_cols]
-    for i in range(1, seq_parts):
-        chosen = jnp.where(seq == i, summed[:, i * kv_cols : (i + 1) * kv_cols], chosen)
-    kvout_ref[...] = chosen
-    small_ref[...] = vec_sum.line_sum()
-
-
-COL_EVENT = 5
-ROW_EVENT = 8
-
-
-def small_scratch(seq_parts, half, block, line_block, dtype):
+    keyval_sum.core_finish()
+    keyval_sum.plane_start()
+    attn_small.plane_start()
+    dx[...] = go[...].astype(f32) + (back - back_mean - normed * back_dot) * rstd[:, 0:1]
+    eout[...] = expand_sum.line_finish()
+    pout[...] = project_sum.line_finish().T
+    stores += [store(dx, dx_hbm.at[0], 1), store(eout, eout_hbm, 2), store(pout, pout_hbm, 3)]
+    for copy in stores[1:]:
+        copy.start()
+    keyval_sum.plane_finish()
+    keyval_sum.line_start()
+    attn_small.line_start()
+    feed_small_ref[...] = feed_small.line_sum()
+    qd_ref[...] = attn_sum.line_finish()
+    summed = keyval_sum.line_finish()
+    kvout_ref[...] = summed
+    attn_small_ref[...] = attn_small.line_sum()
+    for copy in stores:
+        copy.wait()
+
+
+def finish_kernel(
+    parts, out_in, dx_in, e_in, p_in, qd_ref, kv_ref, feed_ref, attn_ref, out_hbm, dx_hbm, e_hbm, p_hbm,
+    wq_ref, wd_ref, wkv_ref, again_ref, ashift_ref, fgain_ref, fshift_ref, qbias_ref, kvbias_ref,
+    dbias_ref, ebias_ref, pbias_ref, out_buf, dx_buf, e_buf, p_buf, in_sem, out_sem,
+):
+    sources, targets = (out_in, dx_in, e_in, p_in), (out_hbm, dx_hbm, e_hbm, p_hbm)
+    held = (out_buf, dx_buf, e_buf, p_buf)
+    incoming = [pltpu.make_async_copy(s, b, in_sem.at[i]) for i, (s, b) in enumerate(zip(sources, held))]
+    outgoing = [pltpu.make_async_copy(b, t, out_sem.at[i]) for i, (b, t) in enumerate(zip(held, targets))]
+    for copy in incoming:
+        copy.start()
+    cols = wq_ref.shape[1]
+    wq_ref[...] = qd_ref[:, 0:cols]
+    wd_ref[...] = qd_ref[:, cols:]
+    summed = kv_ref[...]
+    rest = jnp.zeros((summed.shape[0], 128 - summed.shape[1]), f32)
+    wkv_ref[...] = jnp.concatenate([summed, rest], axis=1).T[0 : summed.shape[1], :]
+    fgain_ref[...] = feed_ref[parts, :]
+    fshift_ref[...] = feed_ref[parts + 1, :]
+    dbias_ref[...] = feed_ref[parts + 2, :]
+    pbias_ref[...] = feed_ref[parts + 2, :]
+    width = feed_ref.shape[1]
+    for i in range(parts):
+        ebias_ref[i * width : (i + 1) * width] = feed_ref[i, :]
+    again_ref[...] = attn_ref[0, :]
+    ashift_ref[...] = attn_ref[1, :]
+    qbias_ref[...] = attn_ref[2, :]
+    kvbias_ref[...] = attn_ref[3, 0 : kvbias_ref.shape[0]]
+    for i in range(len(held)):
+        incoming[i].wait()
+        outgoing[i].start()
+    for copy in outgoing:
+        copy.wait()
+
+
+SIDE_EVENT = 1
+LINE_EVENT = 5
+
+
+def small_scratch(seq_parts, half, block):
     dma = pltpu.SemaphoreType.DMA
     return [
-        pltpu.VMEM(block, dtype), pltpu.VMEM((seq_parts,) + block, dtype),
-        pltpu.VMEM((half,) + line_block, dtype), dma((1,)), dma((1,)), dma((seq_parts - 1,)),
+        pltpu.VMEM(block, f32), pltpu.VMEM(block, f32), pltpu.VMEM((seq_parts,) + block, f32),
+        pltpu.VMEM((half,) + block, f32), dma((1,)), dma((1,)), dma((seq_parts - 1,)),
         dma((seq_parts - 1,)), dma((half - 1,)), dma((half - 1,)),
     ]
 
@@ -786,62 +1030,71 @@
     hidden_units = expand_weight.shape[1]
     chunk = hidden_units // seq_parts
     whole_len = stretch * seq_parts
-    positions = lax.axis_index("seq") * stretch + jnp.arange(stretch, dtype=jnp.int32)
-    half_rot = ROT // 2
-    frequency = 10000.0 ** (-2.0 * jnp.arange(half_rot, dtype=f32) / ROT)
-    angles = frequency[:, None] * positions.astype(f32)[None, :]
     rows, cols = width // dp_parts, width // seq_parts
     col_block, row_block = (rows, chunk), (cols, hidden_units // dp_parts)
-    vec_rows = -(-(seq_parts + 7) // 8) * 8
+    kv_block = (2 * HD // seq_parts, rows)
+    small_block = (-(-(seq_parts + 3) // 8) * 8, width)
     sd, dma = jax.ShapeDtypeStruct, pltpu.SemaphoreType.DMA
 
     def vm(shape, dtype=bf16):
         return pltpu.VMEM(shape, dtype)
 
     in_vmem, in_hbm = pl.BlockSpec(memory_space=pltpu.VMEM), pl.BlockSpec(memory_space=pl.ANY)
-    outs = pl.pallas_call(
+    large = (
+        sd((1, stretch, width), bf16), sd((1, stretch, width), f32), sd(col_block, f32),
+        sd(row_block[::-1], f32),
+    )
+    mids = pl.pallas_call(
         functools.partial(layer_kernel, seq_parts, half),
-        out_shape=(
-            sd((stretch, width), bf16), sd((stretch, width), f32), sd(col_block, f32),
-            sd(row_block[::-1], f32), sd((rows, cols), f32), sd((rows, cols), f32),
-            sd((rows, 2 * HD // seq_parts), f32), sd((vec_rows, width), f32),
-        ),
-        in_specs=[pl.BlockSpec(memory_space=pltpu.SMEM)] + [in_vmem] * 11 + [in_hbm] * 7,
-        out_specs=(in_vmem,) * 8,
+        out_shape=large
+        + (sd((rows, 2 * cols), f32), sd(kv_block, f32), sd(small_block, f32), sd(small_block, f32)),
+        in_specs=[pl.BlockSpec(memory_space=pltpu.SMEM)] + [in_vmem] * 9 + [in_hbm] * 7,
+        out_specs=(in_hbm,) * 4 + (in_vmem,) * 4,
         scratch_shapes=[
             vm((stretch, width)), vm((stretch, width)), vm((width, width)), vm((width, 2 * HD)),
             vm((width, width)), vm((2, width, chunk)), vm((2, chunk, width)),
             vm((stretch, width), f32), vm((stretch, 128), f32), vm((stretch, width)),
             vm((width, stretch)), vm((width, stretch)), vm((width, stretch)),
             vm((stretch, width), f32), vm((width, stretch)), vm((width, stretch)),
-            vm((width, stretch)), vm((width, stretch)), vm((seq_parts, 2 * HD, stretch)),
-            vm((HD, whole_len)), vm((HD + 16, whole_len)), vm((whole_len, 2 * HD)),
-            vm((whole_len, 2 * HD)), vm((whole_len, stretch), f32), vm((whole_len, stretch)),
-            vm((2 * HD, stretch)), vm((2 * HD, 2 * stretch)), vm((whole_len, 2 * HD), f32),
-            vm((seq_parts - 1, stretch, 2 * HD)), vm((seq_parts - 1, stretch, 2 * HD)),
-            vm((2, half, rows, 2 * HD)), vm((vec_rows, width), f32), vm((half, rows, 2 * HD)),
-            dma((9,)), dma((seq_parts - 1,)), dma((seq_parts - 1,)), dma((seq_parts - 1,)),
+            vm((width, stretch)), vm((width, stretch)), vm((stretch, hidden_units)),
+            vm((seq_parts, 2 * HD, stretch)), vm((HD, whole_len)), vm((HD + 16, whole_len)),
+            vm((whole_len, 2 * HD)), vm((whole_len, 2 * HD)), vm((whole_len, stretch), f32),
+            vm((whole_len, stretch)), vm((2 * HD, stretch)), vm((2 * HD, 2 * stretch)),
+            vm((whole_len, 2 * HD), f32), vm((seq_parts - 1, stretch, 2 * HD)),
+            vm((seq_parts - 1, stretch, 2 * HD)), vm((8, chunk), f32), vm((ROT, stretch), f32),
+            vm((stretch, width), f32), vm(col_block, f32), vm(row_block[::-1], f32),
+            dma((9,)), dma((4,)), dma((seq_parts - 1,)), dma((seq_parts - 1,)), dma((seq_parts - 1,)),
             dma((seq_parts - 1,)),
         ]
-        + reduction_scratch(seq_parts, half, col_block, row_block)
+        + tree_scratch(half, col_block)
+        + tree_scratch(half, row_block)
         + reduction_scratch(seq_parts, half, (rows, cols), (rows, cols))
-        + small_scratch(seq_parts, half, (vec_rows, width), (vec_rows, width), f32)
-        + small_scratch(seq_parts, half, (half, rows, 2 * HD), (rows, 2 * HD), bf16),
+        + small_scratch(seq_parts, half, small_block)
+        + small_scratch(seq_parts, half, small_block)
+        + keyval_scratch(seq_parts, half, kv_block),
         compiler_params=pltpu.CompilerParams(
             collective_id=0, has_side_effects=True, vmem_limit_bytes=VMEM_BYTES
         ),
     )(
-        seq_lengths, jnp.cos(angles), jnp.sin(angles), attention_gain[None], attention_shift[None],
-        feed_gain[None], feed_shift[None], query_bias[:, None], keyval_bias[:, None], dense_bias[None],
-        expand_bias.reshape(seq_parts, 1, chunk), project_bias[None], hidden_in[0], out_grad[0],
-        query_weight, keyval_weight, dense_weight, expand_weight, project_weight,
-    )
-    output, input_grad, expand_grad, project_grad, query_grad, dense_grad, keyval_grad, small = outs
-    n = seq_parts
+        seq_lengths, attention_gain, attention_shift, feed_gain, feed_shift, query_bias, keyval_bias,
+        dense_bias, expand_bias, project_bias, hidden_in, out_grad, query_weight, keyval_weight,
+        dense_weight, expand_weight, project_weight,
+    )
+    vectors = (width, width, width, width, width, 2 * HD, width, hidden_units, width)
+    outs = pl.pallas_call(
+        functools.partial(finish_kernel, seq_parts),
+        out_shape=large
+        + (sd((rows, cols), f32), sd((rows, cols), f32), sd((rows, kv_block[0]), f32))
+        + tuple(sd((size,), f32) for size in vectors),
+        in_specs=[in_hbm] * 4 + [in_vmem] * 4,
+        out_specs=(in_hbm,) * 4 + (in_vmem,) * 12,
+        scratch_shapes=[pltpu.VMEM(v.shape, v.dtype) for v in large] + [dma((4,)), dma((4,))],
+    )(*mids)
+    (output, input_grad, expand_grad, project_grad, query_grad, dense_grad, keyval_grad, a_gain, a_shift,
+     f_gain, f_shift, q_bias, kv_bias, d_bias, e_bias, p_bias) = outs
     return (
-        output[None], input_grad[None], small[n + 4], small[n + 5], small[n], small[n + 1], query_grad,
-        small[n + 3], keyval_grad, small[n + 6, : 2 * HD], dense_grad, small[n + 2], expand_grad,
-        small[:n].reshape(hidden_units), project_grad, small[n + 2],
+        output, input_grad, a_gain, a_shift, f_gain, f_shift, query_grad, q_bias, keyval_grad, kv_bias,
+        dense_grad, d_bias, expand_grad, e_bias, project_grad, p_bias,
     )
 
 
@@ -851,6 +1104,7 @@
     return (
         hidden.shape[0] == 1
         and dp_parts == 2 * seq_parts
+        and seq_parts == 4
         and HEADS % seq_parts == 0
         and hidden_units == seq_parts * width
         and width % (16 * dp_parts) == 0

time: 144 us -> 124 us (0.86)
  local copies, waits for them, and re-layouts: 23.9 us -> 3.34 us
    broadcast_in_dim x8 -> x0, local copies, waits for them, and re-layouts: 10.6 us -> none  [the longest x1 1.6 us: fast_device(): query_bias[:, None]]
    unnamed x18 -> x2, local copies, waits for them, and re-layouts: 9.15 us -> 3.34 us
    pallas_call x0 -> x1, Pallas kernels: none -> 4.77 us  [fast_device(): pl.pallas_call(functools.partial(finish_kernel, seq_parts), out_shape=lar...]
    pallas_call x1, Pallas kernels: 118 us -> 115 us  [fast_device(): pl.pallas_call(functools.partial(layer_kernel, seq_parts, half), out_shap...]
    slice x2 -> x0, local copies, waits for them, and re-layouts: 2.35 us -> none  [the longest x1 1.61 us: fast_device(): small[n + 2]]
where the time goes in v3:
time: 124 us
  Pallas kernels  119 us (96%)
  local copies, waits for them, and re-layouts  3.34 us (3%)
  between operations  1.32 us (1%)
    pallas_call x1, Pallas kernels, fast_device(): pl.pallas_call(functools.partial(layer_kernel, seq_parts, half), out_shap...  115 us
    pallas_call x1, Pallas kernels, fast_device(): pl.pallas_call(functools.partial(finish_kernel, seq_parts), out_shape=lar...  4.77 us
    unnamed x2, local copies, waits for them, and re-layouts  3.34 us

profile of v3, /device:TPU:0, one launch (start us, length us, event | category | flops | bytes accessed | tf_op | source)
XLA Modules:
  0.0 124.0 jit_solution(5486158985901891077)
XLA Ops:
  1.3 114.6 %shard_map.288 = (bf16[1,512,768]{2,1,0:T(8,128)(2,1)}, f32[1,512,768]{2,1,0:T(8,128)}, f32[96,768]{1,0:T(8,128)}, f32[384,192]{1,0:T(8,128)}, f32[96,384]{1,0:T...) custom-call(s32[1]{0:T(128)S(6)} %copy.35.refs_0_, f32[768]{0:T(1024)} %refs_1_.1, f32[768]{0:T(1024)} %refs_2_.1, ...), custom_call_target="tpu_custom_call" | custom-call | tf_op jit(solution)/shard_map/pallas_call | solution.py:1047
  115.9 4.8 %shard_map.289 = (bf16[1,512,768]{2,1,0:T(8,128)(2,1)}, f32[1,512,768]{2,1,0:T(8,128)}, f32[96,768]{1,0:T(8,128)}, f32[384,192]{1,0:T(8,128)}, f32[96,192]{1,0:T...) custom-call(bf16[1,512,768]{2,1,0:T(8,128)(2,1)} %get-tuple-element., ...), custom_call_target="tpu_custom_call" | custom-call | tf_op jit(solution)/shard_map/pallas_call | solution.py:1084
  120.7 1.5 %copy.33 = f32[96,32]{0,1:T(8,128)} copy(f32[96,32]{1,0:T(8,128)} %get-tuple-element.72) | data formatting | bytes 24576
  122.2 1.9 %copy.34 = f32[384,192]{0,1:T(8,128)} copy(f32[384,192]{1,0:T(8,128)} %get-tuple-element.78) | data formatting | bytes 589824

commit v4 on v3

--- a/solution.py
+++ b/solution.py
@@ -692,14 +692,12 @@
 
     pl.semaphore_wait(barrier, seq_parts + half - 1)
     loads[2].wait()
-    wq_t = wq[...].T
-    query_bias = column(qbias_ref)
+    query_pre = dot(wq[...].T, attn_t[...]) + column(qbias_ref)
     for hop in range(1, seq_parts):
         kv_copy(hop).start()
     for head in range(HEADS):
         span = slice(head * HD, (head + 1) * HD)
-        rows = dot(wq_t[span, :], attn_t[...]) + query_bias[span, :]
-        query_t[span, :] = (turn(rows, 1.0) * scale).astype(bf16)
+        query_t[span, :] = (turn(query_pre[span, :], 1.0) * scale).astype(bf16)
 
     loads[3].wait()
     token = seq * stretch + lax.broadcasted_iota(jnp.int32, (stretch, 1), 0)
@@ -751,10 +749,6 @@
         def _():
             expand_sum.via_start()
 
-        @pl.when(step == 3)
-        def _():
-            expand_sum.side_start()
-
         expand_sum.core_copy(step).start()
         return carry
 
@@ -776,8 +770,9 @@
         for i in range(2 * half):
             project_sum.made[slot, i % 2, i // 2] = row_grad[:, i * row_cols : (i + 1) * row_cols]
 
-        @pl.when(step == 2)
-        def _():
+        @pl.when(step == 3)
+        def _():
+            expand_sum.side_start()
             project_sum.via_start()
 
         project_sum.core_copy(step).start()
@@ -871,18 +866,21 @@
         def _():
             project_sum.core_finish(2)
             project_sum.core_finish(3)
+
+        @pl.when(index == FIRST_EVENT)
+        def _():
             expand_sum.side_finish()
             expand_sum.line_start()
 
-        @pl.when(index == 2)
+        @pl.when(index == SMALL_EVENT + 0)
         def _():
             feed_small.core_copy().start()
 
-        @pl.when(index == 3)
+        @pl.when(index == SMALL_EVENT + 1)
         def _():
             feed_small.plane_start()
 
-        @pl.when(index == 4)
+        @pl.when(index == SMALL_EVENT + 2)
         def _():
             feed_small.line_start()
 
@@ -955,7 +953,7 @@
     attn_small.plane_start()
     dx[...] = go[...].astype(f32) + (back - back_mean - normed * back_dot) * rstd[:, 0:1]
     eout[...] = expand_sum.line_finish()
-    pout[...] = project_sum.line_finish().T
+    pout[...] = project_sum.line_finish()
     stores += [store(dx, dx_hbm.at[0], 1), store(eout, eout_hbm, 2), store(pout, pout_hbm, 3)]
     for copy in stores[1:]:
         copy.start()
@@ -977,17 +975,23 @@
     dbias_ref, ebias_ref, pbias_ref, out_buf, dx_buf, e_buf, p_buf, in_sem, out_sem,
 ):
     sources, targets = (out_in, dx_in, e_in, p_in), (out_hbm, dx_hbm, e_hbm, p_hbm)
-    held = (out_buf, dx_buf, e_buf, p_buf)
-    incoming = [pltpu.make_async_copy(s, b, in_sem.at[i]) for i, (s, b) in enumerate(zip(sources, held))]
-    outgoing = [pltpu.make_async_copy(b, t, out_sem.at[i]) for i, (b, t) in enumerate(zip(held, targets))]
+    pieces = []
+    for src, buf, dst in zip(sources, (out_buf, dx_buf, e_buf, p_buf), targets):
+        count = 4 if len(src.shape) == 3 else 1
+        size = src.shape[-2] // count
+        for i in range(count):
+            span = pl.ds(i * size, size)
+            pieces.append(
+                [v.at[0, span] if len(v.shape) == 3 else v.at[span] for v in (src, buf, dst)]
+            )
+    incoming = [pltpu.make_async_copy(p[0], p[1], in_sem.at[i]) for i, p in enumerate(pieces)]
+    outgoing = [pltpu.make_async_copy(p[1], p[2], out_sem.at[i]) for i, p in enumerate(pieces)]
     for copy in incoming:
         copy.start()
     cols = wq_ref.shape[1]
     wq_ref[...] = qd_ref[:, 0:cols]
     wd_ref[...] = qd_ref[:, cols:]
-    summed = kv_ref[...]
-    rest = jnp.zeros((summed.shape[0], 128 - summed.shape[1]), f32)
-    wkv_ref[...] = jnp.concatenate([summed, rest], axis=1).T[0 : summed.shape[1], :]
+    wkv_ref[...] = kv_ref[...]
     fgain_ref[...] = feed_ref[parts, :]
     fshift_ref[...] = feed_ref[parts + 1, :]
     dbias_ref[...] = feed_ref[parts + 2, :]
@@ -999,15 +1003,17 @@
     ashift_ref[...] = attn_ref[1, :]
     qbias_ref[...] = attn_ref[2, :]
     kvbias_ref[...] = attn_ref[3, 0 : kvbias_ref.shape[0]]
-    for i in range(len(held)):
+    for i in range(len(pieces)):
         incoming[i].wait()
         outgoing[i].start()
     for copy in outgoing:
         copy.wait()
 
 
-SIDE_EVENT = 1
-LINE_EVENT = 5
+FIRST_EVENT = 3
+SIDE_EVENT = 4
+LINE_EVENT = 8
+SMALL_EVENT = 9
 
 
 def small_scratch(seq_parts, half, block):
@@ -1042,7 +1048,7 @@
     in_vmem, in_hbm = pl.BlockSpec(memory_space=pltpu.VMEM), pl.BlockSpec(memory_space=pl.ANY)
     large = (
         sd((1, stretch, width), bf16), sd((1, stretch, width), f32), sd(col_block, f32),
-        sd(row_block[::-1], f32),
+        sd(row_block, f32),
     )
     mids = pl.pallas_call(
         functools.partial(layer_kernel, seq_parts, half),
@@ -1062,7 +1068,7 @@
             vm((whole_len, stretch)), vm((2 * HD, stretch)), vm((2 * HD, 2 * stretch)),
             vm((whole_len, 2 * HD), f32), vm((seq_parts - 1, stretch, 2 * HD)),
             vm((seq_parts - 1, stretch, 2 * HD)), vm((8, chunk), f32), vm((ROT, stretch), f32),
-            vm((stretch, width), f32), vm(col_block, f32), vm(row_block[::-1], f32),
+            vm((stretch, width), f32), vm(col_block, f32), vm(row_block, f32),
             dma((9,)), dma((4,)), dma((seq_parts - 1,)), dma((seq_parts - 1,)), dma((seq_parts - 1,)),
             dma((seq_parts - 1,)),
         ]
@@ -1084,17 +1090,17 @@
     outs = pl.pallas_call(
         functools.partial(finish_kernel, seq_parts),
         out_shape=large
-        + (sd((rows, cols), f32), sd((rows, cols), f32), sd((rows, kv_block[0]), f32))
+        + (sd((rows, cols), f32), sd((rows, cols), f32), sd(kv_block, f32))
         + tuple(sd((size,), f32) for size in vectors),
         in_specs=[in_hbm] * 4 + [in_vmem] * 4,
         out_specs=(in_hbm,) * 4 + (in_vmem,) * 12,
-        scratch_shapes=[pltpu.VMEM(v.shape, v.dtype) for v in large] + [dma((4,)), dma((4,))],
+        scratch_shapes=[pltpu.VMEM(v.shape, v.dtype) for v in large] + [dma((10,)), dma((10,))],
     )(*mids)
     (output, input_grad, expand_grad, project_grad, query_grad, dense_grad, keyval_grad, a_gain, a_shift,
      f_gain, f_shift, q_bias, kv_bias, d_bias, e_bias, p_bias) = outs
     return (
-        output, input_grad, a_gain, a_shift, f_gain, f_shift, query_grad, q_bias, keyval_grad, kv_bias,
-        dense_grad, d_bias, expand_grad, e_bias, project_grad, p_bias,
+        output, input_grad, a_gain, a_shift, f_gain, f_shift, query_grad, q_bias, keyval_grad.T, kv_bias,
+        dense_grad, d_bias, expand_grad, e_bias, project_grad.T, p_bias,
     )
 
 

time: 124 us -> 111 us (0.90)
  Pallas kernels: 119 us -> 109 us
  local copies, waits for them, and re-layouts: 3.34 us -> 0 us
    pallas_call x1, Pallas kernels: 115 us -> 104 us  [fast_device(): pl.pallas_call(functools.partial(layer_kernel, seq_parts, half), out_shap...]
    unnamed x2 -> x0, local copies, waits for them, and re-layouts: 3.34 us -> none
where the time goes in v4:
time: 111 us; the launch traced here: 110 us
  Pallas kernels  109 us (98%)
  between operations  1.49 us (1%)
    pallas_call x1, Pallas kernels, fast_device(): pl.pallas_call(functools.partial(layer_kernel, seq_parts, half), out_shap...  104 us
    pallas_call x1, Pallas kernels, fast_device(): pl.pallas_call(functools.partial(finish_kernel, seq_parts), out_shape=lar...  4.55 us

profile of v4, /device:TPU:0, one launch (start us, length us, event | category | flops | bytes accessed | tf_op | source)
XLA Modules:
  0.0 110.4 jit_solution(1823756834657015908)
XLA Ops:
  1.3 104.4 %shard_map.288 = (bf16[1,512,768]{2,1,0:T(8,128)(2,1)}, f32[1,512,768]{2,1,0:T(8,128)}, f32[96,768]{1,0:T(8,128)}, f32[192,384]{1,0:T(8,128)}, f32[96,384]{1,0:T...) custom-call(s32[1]{0:T(128)S(6)} %copy.33.refs_0_, f32[768]{0:T(1024)} %refs_1_.1, f32[768]{0:T(1024)} %refs_2_.1, ...), custom_call_target="tpu_custom_call" | custom-call | tf_op jit(solution)/shard_map/pallas_call | solution.py:1053
  105.7 4.5 %shard_map.289 = (bf16[1,512,768]{2,1,0:T(8,128)(2,1)}, f32[1,512,768]{2,1,0:T(8,128)}, f32[96,768]{1,0:T(8,128)}, f32[192,384]{1,0:T(8,128)}, f32[96,192]{1,0:T...) custom-call(bf16[1,512,768]{2,1,0:T(8,128)(2,1)} %get-tuple-element., ...), custom_call_target="tpu_custom_call" | custom-call | tf_op jit(solution)/shard_map/pallas_call | solution.py:1090

commit v5 on v4

--- a/solution.py
+++ b/solution.py
@@ -738,12 +738,11 @@
             expand_sum.made[slot, i % 2, i // 2] = col_grad[i * col_rows : (i + 1) * col_rows, :]
         feed_own[pl.ds(part, 1), :] = dot(ones, grad_upper)[0:1, :]
 
+        dx[...] += dot_nt(grad_upper, we[slot])
+
         @pl.when(step > 0)
         def _():
             expand_sum.core_finish(step - 1)
-
-        base[...] += dot(active, wp[slot])
-        dx[...] += dot_nt(grad_upper, we[slot])
 
         @pl.when(step == 1)
         def _():
@@ -905,6 +904,11 @@
 
         return carry
 
+    def load_again(i):
+        return load(wp_hbm.at[i * chunk : (i + 1) * chunk, :], wp.at[i % 2], 6 + 2 * (i % 2))
+
+    for i in range(2):
+        load_again(i).start()
     lax.fori_loop(0, HEADS, head_step, 0)
 
     def dkv_copy(hop):
@@ -918,13 +922,10 @@
     last = seq_parts - 1
     group_grads(last)
     attn_sum.core_start(last)
-    feed[...] = (base[...] + dot(mix_t[...].T, wd[...])).astype(bf16)
+    grad_attn = dot_nt(gq_t[...].T, wq[...])
     attn_own[2:3, :] = dot_nt(ones, gq_t[...])[0:1, :]
-    grad_attn = dot_nt(gq_t[...].T, wq[...])
     attn_sum.core_finish(last)
     attn_sum.plane_start(last)
-    stores = [store(feed, out_hbm.at[0], 0)]
-    stores[0].start()
     total = dkv[0:stretch, :]
     for hop in range(1, seq_parts):
         dkv_copy(hop).wait()
@@ -944,22 +945,30 @@
     attn_small.core_copy().start()
     attn_sum.sum_finish()
     attn_sum.line_start()
+    keyval_sum.core_finish()
+    keyval_sum.plane_start()
+    attn_small.plane_start()
     back = dx[...] + grad_attn * row(again_ref)
     normed = norm[...]
     back_mean = jnp.mean(back, axis=1, keepdims=True)
     back_dot = jnp.mean(back * normed, axis=1, keepdims=True)
-    keyval_sum.core_finish()
-    keyval_sum.plane_start()
-    attn_small.plane_start()
     dx[...] = go[...].astype(f32) + (back - back_mean - normed * back_dot) * rstd[:, 0:1]
-    eout[...] = expand_sum.line_finish()
-    pout[...] = project_sum.line_finish()
-    stores += [store(dx, dx_hbm.at[0], 1), store(eout, eout_hbm, 2), store(pout, pout_hbm, 3)]
-    for copy in stores[1:]:
-        copy.start()
     keyval_sum.plane_finish()
     keyval_sum.line_start()
     attn_small.line_start()
+    stores = [store(dx, dx_hbm.at[0], 1)]
+    stores[0].start()
+    for i in range(seq_parts):
+        load_again(i).wait()
+        base[...] += dot(active_all[:, i * chunk : (i + 1) * chunk], wp[i % 2])
+        if i + 2 < seq_parts:
+            load_again(i + 2).start()
+    feed[...] = (base[...] + dot(mix_t[...].T, wd[...])).astype(bf16)
+    eout[...] = expand_sum.line_finish()
+    pout[...] = project_sum.line_finish()
+    stores += [store(feed, out_hbm.at[0], 0), store(eout, eout_hbm, 2), store(pout, pout_hbm, 3)]
+    for copy in stores[1:]:
+        copy.start()
     feed_small_ref[...] = feed_small.line_sum()
     qd_ref[...] = attn_sum.line_finish()
     summed = keyval_sum.line_finish()

time: 111 us -> 109 us (0.982)
    pallas_call x1, Pallas kernels: 104 us -> 103 us  [fast_device(): pl.pallas_call(functools.partial(layer_kernel, seq_parts, half), out_shap...]
where the time goes in v5:
time: 109 us
  Pallas kernels  108 us (99%)
  between operations  1.49 us (1%)
    pallas_call x1, Pallas kernels, fast_device(): pl.pallas_call(functools.partial(layer_kernel, seq_parts, half), out_shap...  103 us
    pallas_call x1, Pallas kernels, fast_device(): pl.pallas_call(functools.partial(finish_kernel, seq_parts), out_shape=lar...  4.55 us

profile of v5, /device:TPU:0, one launch (start us, length us, event | category | flops | bytes accessed | tf_op | source)
XLA Modules:
  0.0 109.1 jit_solution(16697424655967775900)
XLA Ops:
  1.3 103.0 %shard_map.288 = (bf16[1,512,768]{2,1,0:T(8,128)(2,1)}, f32[1,512,768]{2,1,0:T(8,128)}, f32[96,768]{1,0:T(8,128)}, f32[192,384]{1,0:T(8,128)}, f32[96,384]{1,0:T...) custom-call(s32[1]{0:T(128)S(6)} %copy.33.refs_0_, f32[768]{0:T(1024)} %refs_1_.1, f32[768]{0:T(1024)} %refs_2_.1, ...), custom_call_target="tpu_custom_call" | custom-call | tf_op jit(solution)/shard_map/pallas_call | solution.py:1062
  104.3 4.5 %shard_map.289 = (bf16[1,512,768]{2,1,0:T(8,128)(2,1)}, f32[1,512,768]{2,1,0:T(8,128)}, f32[96,768]{1,0:T(8,128)}, f32[192,384]{1,0:T(8,128)}, f32[96,192]{1,0:T...) custom-call(bf16[1,512,768]{2,1,0:T(8,128)(2,1)} %get-tuple-element., ...), custom_call_target="tpu_custom_call" | custom-call | tf_op jit(solution)/shard_map/pallas_call | solution.py:1099
